TPU v7x, 8 devices: a whole 2x2x1 slice. The times are simulated.
8 devices in a mesh: dp: 1 (over z), tp: 2 (over y), sp: 4 (over x, core).
Axes of the slice: x: 2, y: 2, z: 1, core: 2. Of those that a mesh axis runs over, the one named last changes fastest.
Arguments:
- x_in: bfloat16 [64, 2048], P('dp')
- seq_lens: int32 [64], P('dp')
- k_cache: bfloat16 [64, 256, 16, 128], P('dp', 'sp', 'tp')
- v_cache: bfloat16 [64, 256, 16, 128], P('dp', 'sp', 'tp')
- ln1_gain: float32 [2048], replicated
- w_qkv: bfloat16 [2048, 3, 16, 128], P(None, None, 'tp')
- w_out: bfloat16 [16, 128, 2048], P('tp')
- ln2_gain: float32 [2048], replicated
- w_up: bfloat16 [2048, 8192], P(None, 'tp')
- w_down: bfloat16 [8192, 2048], P('tp')
Outputs:
- output 1: bfloat16 [64, 2048], P('dp')
- output 2: bfloat16 [64, 256, 16, 128], P('dp', 'sp', 'tp')
- output 3: bfloat16 [64, 256, 16, 128], P('dp', 'sp', 'tp')
All inputs are finite; a program needn't handle non-finite values.
Results may differ from a plain program's by a relative error of at most 0.00568629.
Values sent between devices are 32-bit elements.
A program may use at most 1 GiB of HBM per device.

v0:
```python
import jax
import jax.numpy as jnp
from jax import lax
from jax.sharding import PartitionSpec as P

LN_EPS = 1e-5


def layer_norm(x_f32, gain):
    mean = jnp.mean(x_f32, axis=-1, keepdims=True)
    centred = x_f32 - mean
    variance = jnp.mean(centred * centred, axis=-1, keepdims=True)
    return centred * lax.rsqrt(variance + LN_EPS) * gain


def solution(mesh):
    tp_size = mesh.shape["tp"]

    def local_layer(x_in, seq_lens, k_cache, v_cache, ln1_gain, w_qkv, w_out, ln2_gain, w_up, w_down):
        tok_dev = k_cache.shape[1]
        local_heads = k_cache.shape[2]
        head_dim = k_cache.shape[3]
        heads = local_heads * tp_size
        tp_index = lax.axis_index("tp")
        sp_index = lax.axis_index("sp")
        normed = layer_norm(x_in.astype(jnp.float32), ln1_gain).astype(jnp.bfloat16)
        qkv_proj = jnp.einsum("bd,dchk->bchk", normed, w_qkv, preferred_element_type=jnp.float32).astype(jnp.bfloat16)
        slot_pos = sp_index * tok_dev + jnp.arange(tok_dev)
        slot_hit = (slot_pos[None, :] == seq_lens[:, None])[:, :, None, None]
        k_next = jnp.where(slot_hit, qkv_proj[:, 1][:, None], k_cache)
        v_next = jnp.where(slot_hit, qkv_proj[:, 2][:, None], v_cache)
        head_ids = tp_index * local_heads + jnp.arange(local_heads)
        slopes = jnp.exp2(-8.0 * (head_ids + 1).astype(jnp.float32) / heads)
        scores = jnp.einsum("bhk,bthk->bht", qkv_proj[:, 0], k_next, preferred_element_type=jnp.float32) * head_dim ** -0.5
        distance = (seq_lens[:, None] - slot_pos[None, :]).astype(jnp.float32)
        scores = scores - slopes[None, :, None] * distance[:, None, :]
        is_valid = (slot_pos[None, :] <= seq_lens[:, None])[:, None, :]
        scores = jnp.where(is_valid, scores, -1e30)
        local_max = jnp.max(scores, axis=2)
        weights = jnp.where(is_valid, jnp.exp(scores - local_max[:, :, None]), 0.0)
        local_sum = jnp.sum(weights, axis=2)
        local_out = jnp.einsum("bht,bthk->bhk", weights.astype(jnp.bfloat16), v_next, preferred_element_type=jnp.float32)
        global_max = lax.pmax(local_max, "sp")
        rescale = jnp.exp(local_max - global_max)
        packed = jnp.concatenate([local_out * rescale[:, :, None], (local_sum * rescale)[:, :, None]], axis=2)
        packed = lax.psum(packed, "sp")
        attended = (packed[:, :, :head_dim] / packed[:, :, head_dim:]).astype(jnp.bfloat16)
        attn_part = jnp.einsum("bhk,hkd->bd", attended, w_out, preferred_element_type=jnp.float32)
        residual = x_in.astype(jnp.float32) + lax.psum(attn_part, "tp")
        normed_mid = layer_norm(residual, ln2_gain).astype(jnp.bfloat16)
        hidden = jax.nn.gelu(jnp.dot(normed_mid, w_up, preferred_element_type=jnp.float32), approximate=False).astype(jnp.bfloat16)
        down_part = jnp.dot(hidden, w_down, preferred_element_type=jnp.float32)
        x_out = (residual + lax.psum(down_part, "tp")).astype(jnp.bfloat16)
        return x_out, k_next, v_next

    cache_spec = P("dp", "sp", "tp", None)
    in_specs = (P("dp", None), P("dp"), cache_spec, cache_spec, P(None), P(None, None, "tp", None), P("tp", None, None), P(None), P(None, "tp"), P("tp", None))
    out_specs = (P("dp", None), cache_spec, cache_spec)
    return jax.shard_map(local_layer, mesh=mesh, in_specs=in_specs, out_specs=out_specs, check_vma=False)
```

profile of v0, /device:TPU:0, one launch (start us, length us, event | category | flops | bytes accessed | tf_op | source)
XLA Modules:
  0.0 156.7 jit_solution(15648319125313065526)
XLA Ops:
  7.2 0.0 all-reduce.4.cloned.1.call-start
  7.2 0.7 broadcast_compare_fusion.1
  8.0 0.7 subtract_convert_fusion
  8.7 1.1 convert_reduce_fusion
  9.8 0.0 slice-start
  9.8 1.3 fusion.23
  11.2 0.0 slice-start.1
  11.2 0.0 copy-start
  11.2 7.2 %fusion.6 = bf16[64,3,8,128]{3,0,2,1:T(8,128)(2,1)S(1)} fusion(bf16[2048,3,8,128]{3,2,1,0:T(8,128)(2,1)} %param.15, bf16[64,2048]{1,0:T(8,128)(2,1)} %param.10, f32[2048]{0:T(1024)} %param.14, f32[64]{0:T(128)S(1)} %add_rsqrt_fusion.1, f32[64]{0:T(128)S(1)} %broadcast_multiply_fusion.1), kind=kOutput, calls=%fused_computation.10 | convolution fusion | flops 806158336 | bytes 13246976 | tf_op jit(solution)/shard_map/bd,dchk->bchk/dot_general | solution.py:27
  18.4 0.1 copy.30
  18.5 0.1 copy.29
  18.6 0.0 slice-done
  18.6 0.0 slice-done.1
  18.6 1.0 copy-done
  19.7 6.5 %broadcast_select_fusion = (bf16[64,64,8,128]{3,2,1,0:T(8,128)(2,1)}, bf16[64,64,8,128]{3,2,1,0:T(8,128)(2,1)S(1)}) fusion(bf16[64,64,8,128]{3,2,1,0:T(8,128)(2,1)S(1)} %bitcast.28, pred[64,64]{1,0:T(8,128)(4,1)S(1)} %get-tuple-element.13, bf16[64,8,128]{2,1,0:T(8,128)(2,1)S(1)} %copy.30, bf16[64,64,8,128]{3,2,1,0:T(8,128)(2,1)S(1)} %copy-done, ...), kind=kLoop, calls=%fused_computation.6 | loop fusion | flops 8388608 | bytes 33820672 | tf_op jit(solution)/shard_map/jit(_where)/select_n | solution.py:31
  26.2 0.0 copy-start.1
  26.2 3.4 %copy-done.1 = bf16[64,64,8,128]{3,2,1,0:T(8,128)(2,1)} copy-done((bf16[64,64,8,128]{3,2,1,0:T(8,128)(2,1)}, bf16[64,64,8,128]{3,2,1,0:T(8,128)(2,1)S(1)}, u32[]{:S(2)}) %copy-start.1) | copy-done | bytes 8388632
  29.6 4.4 %fusion.4 = f32[64,8,1,64]{3,2,1,0:T(1,128)S(1)} fusion(bf16[64,64,8,128]{3,2,1,0:T(8,128)(2,1)S(1)} %get-tuple-element.11, bf16[64,8,128,1]{2,0,1,3:T(8,128)(2,1)S(1)} %get-tuple-element.7), kind=kOutput, calls=%fused_computation.4 | convolution fusion | flops 8388608 | bytes 8650752 | tf_op jit(solution)/shard_map/bhk,bthk->bht/dot_general | solution.py:34
  34.0 0.3 fusion.74
  34.3 0.2 fusion.75
  34.5 0.1 copy.32
  34.6 0.1 copy.33
  34.6 8.7 %pmax.7 = f32[64,8]{0,1:T(8,128)S(1)} all-reduce(f32[64,8]{0,1:T(8,128)S(1)} %copy.32), channel_id=1, replica_groups=mesh['dp'=1,'tp'=2,'sp'=4] {'sp'}, use_global_device_ids=true, to_apply=%region_3.4 | all-reduce | flops 512 | bytes 4096 | tf_op jit(solution)/shard_map/pmax | solution.py:43
  43.4 0.0 copy-start.2
  43.4 0.0 copy-start.4
  43.4 5.7 %fusion.2 = f32[64,8,1,128]{3,2,1,0:T(1,128)S(1)} fusion(bf16[64,64,8,128]{3,2,1,0:T(8,128)(2,1)} %get-tuple-element.10, bf16[64,8,64,1]{2,1,0,3:T(8,128)(2,1)S(1)} %get-tuple-element.8), kind=kOutput, calls=%fused_computation.2 | convolution fusion | flops 8388608 | bytes 8716288 | tf_op jit(solution)/shard_map/bht,bthk->bhk/dot_general | solution.py:42
  49.1 0.3 copy.41
  49.4 0.8 pad_maximum_fusion
  50.3 0.0 all-reduce.4.cloned.1.call-update
  50.3 0.0 all-reduce.6.cloned.1.call-start
  50.3 27.6 %all-reduce.4.cloned.1.call-done = f32[64,8,129]{0,1,2:T(8,128)} async-done(((f32[64,8,129]{0,1,2:T(8,128)}), f32[64,8,129]{0,1,2:T(8,128)}) %all-reduce.4.cloned.1.call-update) | async-done | bytes 264208 | tf_op jit(solution)/shard_map/psum | solution.py:46
  77.9 0.7 slice_bitcast_fusion.3
  78.6 1.1 fusion.26
  79.7 3.9 %convolution_bitcast_fusion = f32[64,2048]{1,0:T(8,128)} fusion(bf16[8,128,2048]{2,1,0:T(8,128)(2,1)} %param.16, bf16[64,8,128]{0,1,2:T(8,128)(2,1)S(1)} %fusion.26), kind=kOutput, calls=%fused_computation.8 | convolution fusion | flops 268435456 | bytes 4849664 | tf_op jit(solution)/shard_map/bhk,hkd->bd/dot_general | solution.py:48
  83.6 0.0 all-reduce.6.cloned.1.call-update
  83.6 0.2 all-reduce.8.cloned.1.call-start
  83.8 23.2 %all-reduce.6.cloned.1.call-done = f32[64,2048]{1,0:T(8,128)} async-done(((f32[64,2048]{1,0:T(8,128)}), f32[64,2048]{1,0:T(8,128)}) %all-reduce.6.cloned.1.call-update) | async-done | bytes 524304 | tf_op jit(solution)/shard_map/psum | solution.py:49
  107.1 0.0 copy-done.2
  107.1 1.2 fusion.76
  108.3 1.3 multiply_reduce_fusion
  109.6 0.0 copy-done.4
  109.6 0.0 copy-start.3
  109.6 15.7 %fusion.21 = f32[64,2048]{1,0:T(8,128)} fusion(bf16[4096,2048]{1,0:T(8,128)(2,1)} %param.19, bf16[2048,4096]{1,0:T(8,128)(2,1)} %param.18, f32[2048]{0:T(1024)S(1)} %copy-done.4, f32[64]{0:T(128)S(1)} %add_rsqrt_fusion, f32[64]{0:T(128)S(1)} %broadcast_multiply_fusion, f32[64,2048]{1,0:T(8,128)} %all-reduce.6.cloned.1.call-done, ...), kind=kOutput, calls=%fused_computation.35 | convolution fusion | flops 2165309440 | bytes 34873856 | tf_op jit(solution)/shard_map/dot_general | solution.py:52
  125.3 0.0 all-reduce.8.cloned.1.call-update
  125.3 23.0 %all-reduce.8.cloned.1.call-done = f32[64,2048]{1,0:T(8,128)} async-done(((f32[64,2048]{1,0:T(8,128)}), f32[64,2048]{1,0:T(8,128)}) %all-reduce.8.cloned.1.call-update) | async-done | bytes 524304 | tf_op jit(solution)/shard_map/psum | solution.py:53
  148.3 0.0 copy-done.3
  148.3 1.8 %add_convert_fusion = bf16[64,2048]{1,0:T(8,128)(2,1)} fusion(f32[64,2048]{1,0:T(8,128)} %all-reduce.8.cloned.1.call-done, f32[64,2048]{1,0:T(8,128)S(1)} %copy-done.3, bf16[64,2048]{1,0:T(8,128)(2,1)S(1)} %copy-done.2), kind=kLoop, calls=%fused_computation.42 | loop fusion | flops 524288 | bytes 1572864 | tf_op jit(solution)/shard_map/convert_element_type | solution.py:53
  (10 shorter events, 0.1 us)
Async XLA Ops:
  7.2 70.8 %all-reduce.4.cloned.1.call-start = ((), (), s32[]{:S(2)}) async-start(), calls=%async_computation | async-start | bytes 1056768 | tf_op jit(solution)/shard_map/psum | solution.py:46
  9.8 8.8 %slice-start = ((s8[8388608]{0:T(1024)(128)(4,1)}), s8[4194304]{0:T(1024)(128)(4,1)S(1)}, s32[]{:S(2)}) async-start(s8[8388608]{0:T(1024)(128)(4,1)} %bitcast.27), calls=%async_computation.3 | async-start | bytes 8388608
  11.2 7.4 %slice-start.1 = ((s8[8388608]{0:T(1024)(128)(4,1)}), s8[4194304]{0:T(1024)(128)(4,1)S(1)}, s32[]{:S(2)}) async-start(s8[8388608]{0:T(1024)(128)(4,1)} %bitcast.27), calls=%async_computation.4 | async-start | bytes 8388608
  11.2 8.5 %copy-start = (bf16[64,64,8,128]{3,2,1,0:T(8,128)(2,1)S(1)}, bf16[64,64,8,128]{3,2,1,0:T(8,128)(2,1)}, u32[]{:S(2)}) copy-start(bf16[64,64,8,128]{3,2,1,0:T(8,128)(2,1)} %param.12) | copy-start | bytes 25165828
  26.2 3.4 %copy-start.1 = (bf16[64,64,8,128]{3,2,1,0:T(8,128)(2,1)}, bf16[64,64,8,128]{3,2,1,0:T(8,128)(2,1)S(1)}, u32[]{:S(2)}) copy-start(bf16[64,64,8,128]{3,2,1,0:T(8,128)(2,1)S(1)} %get-tuple-element.11) | copy-start | bytes 25165828
  43.4 63.7 %copy-start.2 = (bf16[64,2048]{1,0:T(8,128)(2,1)S(1)}, bf16[64,2048]{1,0:T(8,128)(2,1)}, u32[]{:S(2)}) copy-start(bf16[64,2048]{1,0:T(8,128)(2,1)} %param.10) | copy-start | bytes 786436
  43.4 66.2 %copy-start.4 = (f32[2048]{0:T(1024)S(1)}, f32[2048]{0:T(1024)}, u32[]{:S(2)}) copy-start(f32[2048]{0:T(1024)} %param.17) | copy-start | bytes 24580
  50.3 56.8 %all-reduce.6.cloned.1.call-start = ((), (), s32[]{:S(2)}) async-start(), calls=%async_computation.1 | async-start | bytes 1048576 | tf_op jit(solution)/shard_map/psum | solution.py:49
  83.6 64.7 %all-reduce.8.cloned.1.call-start = ((), (), s32[]{:S(2)}) async-start(), calls=%async_computation.2 | async-start | bytes 1048576 | tf_op jit(solution)/shard_map/psum | solution.py:53
  109.6 38.8 %copy-start.3 = (f32[64,2048]{1,0:T(8,128)S(1)}, f32[64,2048]{1,0:T(8,128)}, u32[]{:S(2)}) copy-start(f32[64,2048]{1,0:T(8,128)} %all-reduce.6.cloned.1.call-done) | copy-start | bytes 1572868
Sparse Core Ops, SparseCore 0:
  50.4 27.4 all-reduce.3
  83.7 23.2 all-reduce.5
  125.5 22.8 all-reduce.7
where the time goes:
time: 157 us
  waiting for transfers between devices  73.9 us (47%)
  matrix products  36.9 us (24%)
  other arithmetic  17.2 us (11%)
  between operations  13.9 us (9%)
  blocking collectives  8.74 us (6%)
  local copies, waits for them, and re-layouts  5.73 us (4%)
    psum x1, waiting for transfers between devices, local_layer(): packed = lax.psum(packed, 'sp')  27.6 us
    psum x1, waiting for transfers between devices, local_layer(): residual = x_in.astype(jnp.float32) + lax.psum(attn_part, 'tp')  23.2 us
    psum x1, waiting for transfers between devices, local_layer(): x_out = (residual + lax.psum(down_part, 'tp')).astype(jnp.bfloat16)  23 us
    dot_general x1, matrix products, local_layer(): down_part = jnp.dot(hidden, w_down, preferred_element_type=jnp.float32)  15.7 us
    pmax x1, blocking collectives, local_layer(): global_max = lax.pmax(local_max, 'sp')  8.74 us
    dot_general x1, matrix products, local_layer(): jnp.einsum('bd,dchk->bchk', normed, w_qkv, preferred_element_type=jnp.flo...  7.18 us
    select_n x1, other arithmetic, local_layer(): v_next = jnp.where(slot_hit, qkv_proj[:, 2][:, None], v_cache)  6.52 us
    dot_general x1, matrix products, local_layer(): jnp.einsum('bht,bthk->bhk', weights.astype(jnp.bfloat16), v_next, preferr...  5.69 us
  transfers between devices with their start and end apart: 3, of which 3 were waited for; matrix products, arithmetic and copies ran while one was open for 0% of the time, Pallas kernels for 0%

commit v1 on v0

v1 whole, which is shorter than its diff:
```python
import functools

import jax
import jax.numpy as jnp
from jax import lax
from jax.experimental import pallas as pl
from jax.experimental.pallas import tpu as pltpu
from jax.sharding import PartitionSpec as P

LN_EPS = 1e-5
NEG = -1e30
F32 = jnp.float32
BF16 = jnp.bfloat16
MESH = pl.DeviceIdType.MESH

B = 64
D = 2048
NH = 8
HD = 128
T = 64
NQ = 2 * D
CH = 8
CP = 32 // CH
FH = 2048
NUP = 4
NOC = 2


def layer_norm(x_f32, gain):
    mean = jnp.mean(x_f32, axis=-1, keepdims=True)
    centred = x_f32 - mean
    variance = jnp.mean(centred * centred, axis=-1, keepdims=True)
    return centred * lax.rsqrt(variance + LN_EPS) * gain


def attend_kernel(x_hbm, lens_hbm, g_hbm, k_hbm, v_hbm, w_hbm, ko_hbm, vo_hbm, o_ref,
                  x_buf, g_buf, lens, w_buf, k_buf, v_buf, lhs, q_s, k_s, v_s,
                  small_sem, w_sem, kin_sem, vin_sem, kout_sem, vout_sem):
    small = [pltpu.make_async_copy(x_hbm, x_buf, small_sem.at[0]),
             pltpu.make_async_copy(g_hbm, g_buf, small_sem.at[1]),
             pltpu.make_async_copy(lens_hbm, lens, small_sem.at[2])]
    for c in small:
        c.start()
    w_copy = [pltpu.make_async_copy(w_hbm.at[:, i], w_buf.at[i], w_sem.at[i]) for i in range(12)]
    for c in w_copy:
        c.start()

    def kv_in(i):
        rows = pl.ds(i * CP, CP)
        return (pltpu.make_async_copy(k_hbm.at[:, rows], k_buf.at[:, rows], kin_sem.at[i]),
                pltpu.make_async_copy(v_hbm.at[:, rows], v_buf.at[:, rows], vin_sem.at[i]))

    def kv_out(i):
        rows = pl.ds(i * CP, CP)
        return (pltpu.make_async_copy(k_buf.at[:, rows], ko_hbm.at[:, rows], kout_sem.at[i]),
                pltpu.make_async_copy(v_buf.at[:, rows], vo_hbm.at[:, rows], vout_sem.at[i]))

    for i in range(CH):
        for c in kv_in(i):
            c.start()

    for c in small:
        c.wait()
    normed = layer_norm(x_buf[...].astype(F32), g_buf[...]).astype(BF16)
    spread = (lax.broadcasted_iota(jnp.int32, (128, 256), 1) // 2
              == lax.broadcasted_iota(jnp.int32, (128, 256), 0)).astype(BF16)
    odd = lax.broadcasted_iota(jnp.int32, (B, 256), 1) % 2 == 1
    for i in range(D // 128):
        twice = jnp.dot(normed[:, i * 128:(i + 1) * 128], spread, preferred_element_type=F32)
        lhs[0:B, i * 256:(i + 1) * 256] = jnp.where(odd, 0.0, twice).astype(BF16)
        lhs[B:2 * B, i * 256:(i + 1) * 256] = jnp.where(odd, twice, 0.0).astype(BF16)

    w_flat = w_buf.reshape(12, NQ, HD)
    for i in range(0, 12, 2):
        w_copy[i].wait()
        w_copy[i + 1].wait()
        two = jnp.concatenate([w_flat[i], w_flat[i + 1]], axis=1)
        res = jnp.dot(lhs[...], two, preferred_element_type=F32)
        for n in range(2):
            part, pair = divmod(i + n, 4)
            for parity in range(2):
                h = 2 * pair + parity
                val = res[parity * B:(parity + 1) * B, n * HD:(n + 1) * HD]
                if part == 0:
                    base = (h // 4) * 8 + h % 4
                    q_s[pl.ds(base, 32, stride=16), :] = val[0:32]
                    q_s[pl.ds(base + 4, 32, stride=16), :] = val[32:64]
                else:
                    (k_s if part == 1 else v_s)[pl.ds(h, B, stride=NH), :] = val

    sp = lax.axis_index("sp")
    tp = lax.axis_index("tp")
    row = lax.broadcasted_iota(jnp.int32, (16, 1), 0)
    head = (row // 8) * 4 + row % 4
    slope = jnp.exp2(-8.0 * (tp * NH + head + 1).astype(F32) / (2 * NH))
    col = lax.broadcasted_iota(jnp.int32, (16, NH * T), 1)
    own_head = col % NH == (lax.broadcasted_iota(jnp.int32, (16, NH * T), 0) // 8) * 4 \
        + lax.broadcasted_iota(jnp.int32, (16, NH * T), 0) % 4
    pos = sp * T + col // NH
    pos = jnp.where(own_head, pos, 1 << 20)
    second = row % 8 >= 4
    second_q = lax.broadcasted_iota(jnp.int32, (16, HD), 0) % 8 >= 4
    second_o = lax.broadcasted_iota(jnp.int32, (8, HD), 0) >= 4
    upper = lax.broadcasted_iota(jnp.int32, (16, HD), 0) >= 8
    lane = lax.broadcasted_iota(jnp.int32, (16, HD), 1)

    def insert(buf, new, half, j):
        b = half * 32 + j
        slot = lens[b] - sp * T
        held = jnp.logical_and(slot >= 0, slot < T)
        at = jnp.clip(slot, 0, T - 1)
        rows = pl.ds(pl.multiple_of((at // 2) * 16, 16), 16)
        fresh = new[pl.ds(pl.multiple_of(b * NH, NH), NH), :]
        fresh = jnp.concatenate([fresh, fresh], axis=0)
        keep = jnp.where(held, at % 2, 2)
        old = buf[half, j, rows, :].astype(F32)
        mine = upper.astype(jnp.int32) == keep
        buf[half, j, rows, :] = jnp.where(mine, fresh, old).astype(BF16)

    def chunk(i, stats):
        for c in kv_in(i):
            c.wait()
        for n in range(CP):
            for half in range(2):
                insert(k_buf, k_s, half, i * CP + n)
                insert(v_buf, v_s, half, i * CP + n)
        scores = []
        for n in range(CP):
            j = i * CP + n
            q = q_s[pl.ds(pl.multiple_of(j * 16, 16), 16), :]
            q2 = jnp.concatenate([jnp.where(second_q, 0.0, q), jnp.where(second_q, q, 0.0)], axis=1).astype(BF16)
            k2 = jnp.concatenate([k_buf[0, j], k_buf[1, j]], axis=1)
            scores.append(lax.dot_general(q2, k2, (((1,), (1,)), ((), ())), preferred_element_type=F32))
        weights = []
        for n in range(CP):
            j = i * CP + n
            length = jnp.where(second, lens[32 + j], lens[j])
            valid = pos <= length
            s = scores[n] * HD ** -0.5 - slope * (length - pos).astype(F32)
            s = jnp.where(valid, s, NEG)
            top = jnp.max(s, axis=1, keepdims=True)
            p = jnp.where(valid, jnp.exp(s - top), 0.0)
            total = jnp.sum(p, axis=1, keepdims=True)
            weights.append(p.astype(BF16))
            stats = jnp.where(lane == j, top, jnp.where(lane == 64 + j, total, stats))
        for n in range(CP):
            j = i * CP + n
            v2 = jnp.concatenate([v_buf[0, j], v_buf[1, j]], axis=1)
            o = jnp.dot(weights[n], v2, preferred_element_type=F32)
            for c in range(2):
                piece = jnp.where(second_o, o[c * 8:(c + 1) * 8, HD:], o[c * 8:(c + 1) * 8, :HD])
                o_ref[c, i // (CH // 2), pl.ds(pl.multiple_of((j % 16) * 8, 8), 8), :] = piece
        for c in kv_out(i):
            c.start()
        return stats

    stats = lax.fori_loop(0, CH, chunk, jnp.zeros((16, HD), F32))
    for c in range(2):
        for x in range(2):
            o_ref[c, x, 128:136, :] = stats[c * 8:(c + 1) * 8]
    for i in range(CH):
        for c in kv_out(i):
            c.wait()


def rest_kernel(o_ref, x_hbm, g_hbm, wo_hbm, wu_hbm, wd_hbm, out_ref,
                x_buf, g_buf, wo_buf, wu_buf, wd_buf, o_recv, att, a_send, a_recv, y_send, y_recv, r_buf,
                hid, d_send, d_recv, z_send, z_recv, f_send, f_recv,
                in_sem, wo_sem, wu_sem, wd_sem, o_ss, o_rs, a_ss, a_rs, y_ss, y_rs, r_ss, r_rs,
                d_ss, d_rs, z_ss, z_rs, f_ss, f_rs):
    sp = lax.axis_index("sp")
    tp = lax.axis_index("tp")
    x = sp // 2
    c = sp % 2
    core = {"sp": x * 2 + (1 - c)}
    flip = {"sp": (1 - x) * 2 + c}
    other_tp = {"tp": 1 - tp}
    half = D // 2
    w = half // NOC

    def remote(src, dst, ss, rs, dev):
        return pltpu.make_async_remote_copy(src_ref=src, dst_ref=dst, send_sem=ss, recv_sem=rs, device_id=dev,
                                            device_id_type=MESH)

    wo_copy, wd_copy = [], []
    for n in range(2):
        cols = pl.ds(pl.multiple_of(((1 - c) if n == 0 else c) * half, half), half)
        wo_copy.append(pltpu.make_async_copy(wo_hbm.at[pl.ds(pl.multiple_of(c * 512, 512), 512), cols], wo_buf.at[n],
                                             wo_sem.at[n]))
        for k in range(NOC):
            cols = pl.ds(pl.multiple_of(((1 - c) if n == 0 else c) * half + k * w, w), w)
            wd_copy.append(pltpu.make_async_copy(wd_hbm.at[pl.ds(pl.multiple_of(c * FH, FH), FH), cols],
                                                 wd_buf.at[n * NOC + k], wd_sem.at[n * NOC + k]))
    wu_copy = [pltpu.make_async_copy(wu_hbm.at[:, pl.ds(pl.multiple_of(c * FH + k * (FH // NUP), FH // NUP), FH // NUP)],
                                     wu_buf.at[k], wu_sem.at[k]) for k in range(NUP)]
    in_copy = [pltpu.make_async_copy(g_hbm, g_buf, in_sem.at[0])]
    for n in range(2):
        in_copy.append(pltpu.make_async_copy(
            x_hbm.at[pl.ds(pl.multiple_of(n * 32 + x * 16, 16), 16), pl.ds(pl.multiple_of(c * half, half), half)],
            x_buf.at[n], in_sem.at[1 + n]))
    for cp in wo_copy + in_copy + wu_copy + wd_copy:
        cp.start()

    barrier = pltpu.get_barrier_semaphore()
    for rel in range(1, 4):
        pl.semaphore_signal(barrier, inc=1, device_id={"sp": (sp + rel) % 4}, device_id_type=MESH)
    pl.semaphore_signal(barrier, inc=1, device_id=other_tp, device_id_type=MESH)
    pl.semaphore_wait(barrier, 4)

    o_copy = []
    for rel in range(1, 4):
        peer = (sp + rel) % 4
        o_copy.append(remote(o_ref.at[peer % 2, peer // 2], o_recv.at[rel - 1], o_ss.at[rel - 1], o_rs.at[rel - 1],
                             {"sp": peer}))
    for cp in o_copy:
        cp.start()
    for cp in o_copy:
        cp.wait()
    parts = [o_ref.at[c, x]] + [o_recv.at[n] for n in range(3)]
    shift = (HD - 16 * x) % HD
    tops = [pltpu.roll(p[128:136, :], shift, 1) for p in parts]
    sums = [pltpu.roll(t, 64, 1) for t in tops]
    top = functools.reduce(jnp.maximum, tops)
    scale = [jnp.exp(t - top) for t in tops]
    total = functools.reduce(jnp.add, [a * s for a, s in zip(scale, sums)])
    scale = [a / total for a in scale]
    for j in range(16):
        acc = None
        for a, p in zip(scale, parts):
            term = p[j * 8:(j + 1) * 8, :] * a[:, j:j + 1]
            acc = term if acc is None else acc + term
        att[j * 8:(j + 1) * 8, :] = acc

    rows = []
    for bb in range(2):
        rows.append(jnp.concatenate([att[pl.ds(bb * 4 + h, 16, stride=8), :] for h in range(4)], axis=1))
    attended = jnp.concatenate(rows, axis=0).astype(BF16)
    wo_copy[0].wait()
    a_copy = []
    for k in range(NOC):
        a_send[k] = jnp.dot(attended, wo_buf[0, :, k * w:(k + 1) * w], preferred_element_type=F32)
        a_copy.append(remote(a_send.at[k], a_recv.at[k], a_ss.at[k], a_rs.at[k], core))
        a_copy[k].start()
    wo_copy[1].wait()
    own = [jnp.dot(attended, wo_buf[1, :, k * w:(k + 1) * w], preferred_element_type=F32) for k in range(NOC)]
    y_copy = []
    for k in range(NOC):
        a_copy[k].wait()
        y_send[k] = own[k] + a_recv[k]
        y_copy.append(remote(y_send.at[k], y_recv.at[k], y_ss.at[k], y_rs.at[k], other_tp))
        y_copy[k].start()
    for cp in in_copy:
        cp.wait()
    x_in = jnp.concatenate([x_buf[0], x_buf[1]], axis=0).astype(F32)
    r_copy = []
    for k in range(NOC):
        y_copy[k].wait()
        r_buf[c, k] = x_in[:, k * w:(k + 1) * w] + (y_send[k] + y_recv[k])
        r_copy.append(remote(r_buf.at[c, k], r_buf.at[c, k], r_ss.at[k], r_rs.at[k], core))
        r_copy[k].start()
    for cp in r_copy:
        cp.wait()

    res = jnp.concatenate([r_buf[n, k] for n in range(2) for k in range(NOC)], axis=1)
    normed = layer_norm(res, g_buf[...]).astype(BF16)
    fw = FH // NUP
    for k in range(NUP):
        wu_copy[k].wait()
        u = jnp.dot(normed, wu_buf[k], preferred_element_type=F32)
        hid[:, k * fw:(k + 1) * fw] = (0.5 * u * (1.0 + lax.erf(u * 0.5 ** 0.5))).astype(BF16)
    d_copy = []
    for k in range(NOC):
        wd_copy[k].wait()
        d_send[k] = jnp.dot(hid[...], wd_buf[k], preferred_element_type=F32)
        d_copy.append(remote(d_send.at[k], d_recv.at[k], d_ss.at[k], d_rs.at[k], core))
        d_copy[k].start()
    z_copy = []
    for k in range(NOC):
        wd_copy[NOC + k].wait()
        mine = jnp.dot(hid[...], wd_buf[NOC + k], preferred_element_type=F32)
        d_copy[k].wait()
        z_send[k] = mine + d_recv[k]
        z_copy.append(remote(z_send.at[k], z_recv.at[k], z_ss.at[k], z_rs.at[k], other_tp))
        z_copy[k].start()

    def put(block, where, cc, k):
        for n in range(2):
            out_ref[pl.ds(pl.multiple_of(n * 32 + where * 16, 16), 16),
                    pl.ds(pl.multiple_of(cc * half + k * w, w), w)] = block[n * 16:(n + 1) * 16].astype(BF16)

    near, far, fwd = [], [], []
    for k in range(NOC):
        z_copy[k].wait()
        val = r_buf[c, k] + (z_send[k] + z_recv[k])
        f_send[k] = val
        far.append(remote(f_send.at[k], f_recv.at[1, k], f_ss.at[1, k], f_rs.at[1, k], flip))
        far[k].start()
        near.append(remote(f_send.at[k], f_recv.at[0, k], f_ss.at[0, k], f_rs.at[0, k], core))
        near[k].start()
        put(val, x, c, k)
    for k in range(NOC):
        far[k].wait()
        fwd.append(remote(f_recv.at[1, k], f_recv.at[2, k], f_ss.at[2, k], f_rs.at[2, k], core))
        fwd[k].start()
        put(f_recv[1, k], 1 - x, c, k)
    for k in range(NOC):
        near[k].wait()
        put(f_recv[0, k], x, 1 - c, k)
    for k in range(NOC):
        fwd[k].wait()
        put(f_recv[2, k], 1 - x, 1 - c, k)


def solution(mesh):
    def hbm(a):
        return pltpu.with_memory_space_constraint(a, pltpu.HBM)

    in_hbm = pl.BlockSpec(memory_space=pltpu.HBM)
    in_vmem = pl.BlockSpec(memory_space=pltpu.VMEM)
    dma = pltpu.SemaphoreType.DMA

    def local_layer(x_in, seq_lens, k_cache, v_cache, ln1_gain, w_qkv, w_out, ln2_gain, w_up, w_down):
        caches = [hbm(a.reshape(2, B // 2, T * NH, HD)) for a in (k_cache, v_cache)]
        cache_type = jax.ShapeDtypeStruct((2, B // 2, T * NH, HD), BF16)
        k_next, v_next, parts = pl.pallas_call(
            attend_kernel,
            out_shape=[cache_type, cache_type, jax.ShapeDtypeStruct((2, 2, 136, HD), F32)],
            in_specs=[in_hbm] * 6,
            out_specs=[in_hbm, in_hbm, in_vmem],
            scratch_shapes=[
                pltpu.VMEM((B, D), BF16), pltpu.VMEM((1, D), F32), pltpu.SMEM((B,), jnp.int32),
                pltpu.VMEM((12, D, 2, HD), BF16),
                pltpu.VMEM((2, B // 2, T * NH, HD), BF16), pltpu.VMEM((2, B // 2, T * NH, HD), BF16),
                pltpu.VMEM((2 * B, NQ), BF16),
                pltpu.VMEM((B * NH, HD), F32), pltpu.VMEM((B * NH, HD), F32), pltpu.VMEM((B * NH, HD), F32),
                dma((3,)), dma((12,)), dma((CH,)), dma((CH,)), dma((CH,)), dma((CH,)),
            ],
            compiler_params=pltpu.CompilerParams(vmem_limit_bytes=44 * 1024 * 1024),
            name="attend",
        )(hbm(x_in), hbm(seq_lens), hbm(ln1_gain.reshape(1, D)), *caches, hbm(w_qkv.reshape(D, 12, 2, HD)))
        w = D // 2 // NOC
        x_out = pl.pallas_call(
            rest_kernel,
            out_shape=jax.ShapeDtypeStruct((B, D), BF16),
            in_specs=[in_vmem] + [in_hbm] * 5,
            out_specs=in_vmem,
            scratch_shapes=[
                pltpu.VMEM((2, 16, D // 2), BF16), pltpu.VMEM((1, D), F32),
                pltpu.VMEM((2, 512, D // 2), BF16), pltpu.VMEM((NUP, D, FH // NUP), BF16),
                pltpu.VMEM((2 * NOC, FH, w), BF16),
                pltpu.VMEM((3, 136, HD), F32), pltpu.VMEM((128, HD), F32),
                pltpu.VMEM((NOC, 32, w), F32), pltpu.VMEM((NOC, 32, w), F32),
                pltpu.VMEM((NOC, 32, w), F32), pltpu.VMEM((NOC, 32, w), F32),
                pltpu.VMEM((2, NOC, 32, w), F32),
                pltpu.VMEM((32, FH), BF16),
                pltpu.VMEM((NOC, 32, w), F32), pltpu.VMEM((NOC, 32, w), F32),
                pltpu.VMEM((NOC, 32, w), F32), pltpu.VMEM((NOC, 32, w), F32),
                pltpu.VMEM((NOC, 32, w), F32), pltpu.VMEM((3, NOC, 32, w), F32),
                dma((3,)), dma((2,)), dma((NUP,)), dma((2 * NOC,)), dma((3,)), dma((3,)),
                dma((NOC,)), dma((NOC,)), dma((NOC,)), dma((NOC,)), dma((NOC,)), dma((NOC,)),
                dma((NOC,)), dma((NOC,)), dma((NOC,)), dma((NOC,)), dma((3, NOC)), dma((3, NOC)),
            ],
            compiler_params=pltpu.CompilerParams(vmem_limit_bytes=32 * 1024 * 1024, collective_id=0,
                                                 has_side_effects=True),
            name="rest",
        )(parts, hbm(x_in), hbm(ln2_gain.reshape(1, D)), hbm(w_out.reshape(NH * HD, D)), hbm(w_up), hbm(w_down))
        return x_out, k_next.reshape(k_cache.shape), v_next.reshape(v_cache.shape)

    cache_spec = P("dp", "sp", "tp", None)
    in_specs = (P("dp", None), P("dp"), cache_spec, cache_spec, P(None), P(None, None, "tp", None), P("tp", None, None), P(None), P(None, "tp"), P("tp", None))
    out_specs = (P("dp", None), cache_spec, cache_spec)
    return jax.shard_map(local_layer, mesh=mesh, in_specs=in_specs, out_specs=out_specs, check_vma=False)
```

time: 157 us -> 52.2 us (0.33)
  waiting for transfers between devices: 73.9 us -> 0 us
  Pallas kernels: 0 us -> 50.7 us
  matrix products: 36.9 us -> 0 us
  other arithmetic: 17.2 us -> 0 us
  between operations: 13.9 us -> 0.65 us
  blocking collectives: 8.74 us -> 0 us
  local copies, waits for them, and re-layouts: 5.73 us -> 0.71 us
    psum x3 -> x0, waiting for transfers between devices: 73.8 us -> none  [the longest x1 27.6 us: local_layer(): packed = lax.psum(packed, 'sp')]
    pallas_call x0 -> x2, Pallas kernels: none -> 50.7 us  [the longest x1 29.3 us: local_layer(): pl.pallas_call(rest_kernel, out_shape=jax.ShapeDtypeStruct((B, D), BF16),...]
    dot_general x5 -> x0, matrix products: 36.9 us -> none  [the longest x1 15.7 us: local_layer(): down_part = jnp.dot(hidden, w_down, preferred_element_type=jnp.float32)]
    pmax x1 -> x0, blocking collectives: 8.74 us -> none  [local_layer(): global_max = lax.pmax(local_max, 'sp')]
    select_n x1 -> x0, other arithmetic: 6.52 us -> none  [local_layer(): v_next = jnp.where(slot_hit, qkv_proj[:, 2][:, None], v_cache)]
    reduce_sum x4 -> x0, other arithmetic: 4.9 us -> none  [the longest x2 2.61 us: layer_norm(): variance = jnp.mean(centred * centred, axis=-1, keepdims=True)]
    convert_element_type x4 -> x0, other arithmetic: 3.88 us -> none  [the longest x1 1.81 us: local_layer(): x_out = (residual + lax.psum(down_part, 'tp')).astype(jnp.bfloat16)]
    unnamed x14 -> x1, local copies, waits for them, and re-layouts: 4.45 us -> 0.71 us
  transfers between devices with their start and end apart: 3 -> 0, of which waited for: 3 -> 0; matrix products, arithmetic and copies ran while one was open for 0% -> 0% of each run, Pallas kernels for 0% -> 0%
where the time goes in v1:
time: 52.2 us; the launch traced here: 52.1 us
  Pallas kernels  50.7 us (97%)
  local copies, waits for them, and re-layouts  0.71 us (1%)
  between operations  0.65 us (1%)
    pallas_call x1, Pallas kernels, local_layer(): pl.pallas_call(rest_kernel, out_shape=jax.ShapeDtypeStruct((B, D), BF16),...  29.3 us
    pallas_call x1, Pallas kernels, local_layer(): pl.pallas_call(attend_kernel, out_shape=[cache_type, cache_type, jax.Shap...  21.4 us

profile of v1, /device:TPU:0, one launch (start us, length us, event | category | flops | bytes accessed | tf_op | source)
XLA Modules:
  0.0 52.1 jit_solution(16748728445963291726)
XLA Ops:
  0.6 21.4 %attend.1 = (bf16[2,32,512,128]{3,2,1,0:T(8,128)(2,1)}, bf16[2,32,512,128]{3,2,1,0:T(8,128)(2,1)}, f32[2,2,136,128]{3,2,1,0:T(8,128)S(1)}) custom-call(bf16[64,2048]{1,0:T(8,128)(2,1)} %x_hbm.3, s32[64]{0:T(128)} %lens_hbm.1, f32[1,2048]{1,0:T(1,128)} %bitcast.12, bf16[2,32,512,128]{3,2,1,0:T(8,128)(2,1)} %bitcast.9, bf16[2,32,512,128]{3,2,1,0:T(8,128)(2,1)} %bitcast.10, ...), custom_call_target="tpu_custom_call" | custom-call | tf_op jit(solution)/shard_map/attend/pallas_call | solution.py:325
  22.1 29.3 %rest.1 = bf16[64,2048]{1,0:T(8,128)(2,1)S(1)} custom-call(f32[2,2,136,128]{3,2,1,0:T(8,128)S(1)} %get-tuple-element.6.o_ref, bf16[64,2048]{1,0:T(8,128)(2,1)} %x_hbm.3, f32[1,2048]{1,0:T(1,128)} %bitcast.13, bf16[1024,2048]{1,0:T(8,128)(2,1)} %bitcast.11, bf16[2048,4096]{1,0:T(8,128)(2,1)} %wu_hbm.1, bf16[4096,2048]{1,0:T(8,128)(2,1)} %wd_hbm.1), custom_call_target="tpu_custom_call" | custom-call | tf_op jit(solution)/shard_map/rest/pallas_call | solution.py:342
  51.4 0.7 %copy.14 = bf16[64,2048]{1,0:T(8,128)(2,1)} copy(bf16[64,2048]{1,0:T(8,128)(2,1)S(1)} %rest.1) | data formatting | bytes 524288

commit v2 on v1

--- a/solution.py
+++ b/solution.py
@@ -33,32 +33,12 @@
     return centred * lax.rsqrt(variance + LN_EPS) * gain
 
 
-def attend_kernel(x_hbm, lens_hbm, g_hbm, k_hbm, v_hbm, w_hbm, ko_hbm, vo_hbm, o_ref,
-                  x_buf, g_buf, lens, w_buf, k_buf, v_buf, lhs, q_s, k_s, v_s,
-                  small_sem, w_sem, kin_sem, vin_sem, kout_sem, vout_sem):
+def prepare_kernel(x_hbm, g_hbm, w_hbm, w_out, lhs, x_buf, g_buf, small_sem, w_sem):
     small = [pltpu.make_async_copy(x_hbm, x_buf, small_sem.at[0]),
-             pltpu.make_async_copy(g_hbm, g_buf, small_sem.at[1]),
-             pltpu.make_async_copy(lens_hbm, lens, small_sem.at[2])]
-    for c in small:
+             pltpu.make_async_copy(g_hbm, g_buf, small_sem.at[1])]
+    w_copy = [pltpu.make_async_copy(w_hbm.at[:, i], w_out.at[i], w_sem.at[i]) for i in range(12)]
+    for c in small + w_copy:
         c.start()
-    w_copy = [pltpu.make_async_copy(w_hbm.at[:, i], w_buf.at[i], w_sem.at[i]) for i in range(12)]
-    for c in w_copy:
-        c.start()
-
-    def kv_in(i):
-        rows = pl.ds(i * CP, CP)
-        return (pltpu.make_async_copy(k_hbm.at[:, rows], k_buf.at[:, rows], kin_sem.at[i]),
-                pltpu.make_async_copy(v_hbm.at[:, rows], v_buf.at[:, rows], vin_sem.at[i]))
-
-    def kv_out(i):
-        rows = pl.ds(i * CP, CP)
-        return (pltpu.make_async_copy(k_buf.at[:, rows], ko_hbm.at[:, rows], kout_sem.at[i]),
-                pltpu.make_async_copy(v_buf.at[:, rows], vo_hbm.at[:, rows], vout_sem.at[i]))
-
-    for i in range(CH):
-        for c in kv_in(i):
-            c.start()
-
     for c in small:
         c.wait()
     normed = layer_norm(x_buf[...].astype(F32), g_buf[...]).astype(BF16)
@@ -69,12 +49,32 @@
         twice = jnp.dot(normed[:, i * 128:(i + 1) * 128], spread, preferred_element_type=F32)
         lhs[0:B, i * 256:(i + 1) * 256] = jnp.where(odd, 0.0, twice).astype(BF16)
         lhs[B:2 * B, i * 256:(i + 1) * 256] = jnp.where(odd, twice, 0.0).astype(BF16)
-
-    w_flat = w_buf.reshape(12, NQ, HD)
+    for c in w_copy:
+        c.wait()
+
+
+def attend_kernel(lhs, w_ref, lens_hbm, k_hbm, v_hbm, ko_hbm, vo_hbm, o_ref,
+                  lens, k_buf, v_buf, q_s, k_s, v_s,
+                  small_sem, kin_sem, vin_sem, kout_sem, vout_sem):
+    lens_copy = pltpu.make_async_copy(lens_hbm, lens, small_sem)
+    lens_copy.start()
+
+    def kv_in(i):
+        rows = pl.ds(i * CP, CP)
+        return (pltpu.make_async_copy(k_hbm.at[:, rows], k_buf.at[:, rows], kin_sem.at[i]),
+                pltpu.make_async_copy(v_hbm.at[:, rows], v_buf.at[:, rows], vin_sem.at[i]))
+
+    def kv_out(i):
+        rows = pl.ds(i * CP, CP)
+        return (pltpu.make_async_copy(k_buf.at[:, rows], ko_hbm.at[:, rows], kout_sem.at[i]),
+                pltpu.make_async_copy(v_buf.at[:, rows], vo_hbm.at[:, rows], vout_sem.at[i]))
+
+    for i in range(CH):
+        for c in kv_in(i):
+            c.start()
+
     for i in range(0, 12, 2):
-        w_copy[i].wait()
-        w_copy[i + 1].wait()
-        two = jnp.concatenate([w_flat[i], w_flat[i + 1]], axis=1)
+        two = jnp.concatenate([w_ref[i], w_ref[i + 1]], axis=1)
         res = jnp.dot(lhs[...], two, preferred_element_type=F32)
         for n in range(2):
             part, pair = divmod(i + n, 4)
@@ -87,6 +87,7 @@
                     q_s[pl.ds(base + 4, 32, stride=16), :] = val[32:64]
                 else:
                     (k_s if part == 1 else v_s)[pl.ds(h, B, stride=NH), :] = val
+    lens_copy.wait()
 
     sp = lax.axis_index("sp")
     tp = lax.axis_index("tp")
@@ -322,22 +323,29 @@
     def local_layer(x_in, seq_lens, k_cache, v_cache, ln1_gain, w_qkv, w_out, ln2_gain, w_up, w_down):
         caches = [hbm(a.reshape(2, B // 2, T * NH, HD)) for a in (k_cache, v_cache)]
         cache_type = jax.ShapeDtypeStruct((2, B // 2, T * NH, HD), BF16)
+        w_split, lhs = pl.pallas_call(
+            prepare_kernel,
+            out_shape=[pltpu.VMEM((12, D, 2, HD), BF16), pltpu.VMEM((2 * B, NQ), BF16)],
+            in_specs=[in_hbm] * 3,
+            out_specs=[in_vmem, in_vmem],
+            scratch_shapes=[pltpu.VMEM((B, D), BF16), pltpu.VMEM((1, D), F32), dma((2,)), dma((12,))],
+            compiler_params=pltpu.CompilerParams(vmem_limit_bytes=16 * 1024 * 1024),
+            name="prepare",
+        )(hbm(x_in), hbm(ln1_gain.reshape(1, D)), hbm(w_qkv.reshape(D, 12, 2, HD)))
         k_next, v_next, parts = pl.pallas_call(
             attend_kernel,
             out_shape=[cache_type, cache_type, jax.ShapeDtypeStruct((2, 2, 136, HD), F32)],
-            in_specs=[in_hbm] * 6,
+            in_specs=[in_vmem] * 2 + [in_hbm] * 3,
             out_specs=[in_hbm, in_hbm, in_vmem],
             scratch_shapes=[
-                pltpu.VMEM((B, D), BF16), pltpu.VMEM((1, D), F32), pltpu.SMEM((B,), jnp.int32),
-                pltpu.VMEM((12, D, 2, HD), BF16),
+                pltpu.SMEM((B,), jnp.int32),
                 pltpu.VMEM((2, B // 2, T * NH, HD), BF16), pltpu.VMEM((2, B // 2, T * NH, HD), BF16),
-                pltpu.VMEM((2 * B, NQ), BF16),
                 pltpu.VMEM((B * NH, HD), F32), pltpu.VMEM((B * NH, HD), F32), pltpu.VMEM((B * NH, HD), F32),
-                dma((3,)), dma((12,)), dma((CH,)), dma((CH,)), dma((CH,)), dma((CH,)),
+                dma, dma((CH,)), dma((CH,)), dma((CH,)), dma((CH,)),
             ],
-            compiler_params=pltpu.CompilerParams(vmem_limit_bytes=44 * 1024 * 1024),
+            compiler_params=pltpu.CompilerParams(vmem_limit_bytes=36 * 1024 * 1024),
             name="attend",
-        )(hbm(x_in), hbm(seq_lens), hbm(ln1_gain.reshape(1, D)), *caches, hbm(w_qkv.reshape(D, 12, 2, HD)))
+        )(lhs, w_split.reshape(12, NQ, HD), hbm(seq_lens), *caches)
         w = D // 2 // NOC
         x_out = pl.pallas_call(
             rest_kernel,

time: 52.2 us -> 48.5 us (0.929)
  Pallas kernels: 50.7 us -> 47.1 us
    pallas_call x1, Pallas kernels: 21.4 us -> 13 us  [local_layer(): pl.pallas_call(attend_kernel, out_shape=[cache_type, cache_type, jax.Shap...]
    pallas_call x0 -> x1, Pallas kernels: none -> 4.8 us  [local_layer(): pl.pallas_call(prepare_kernel, out_shape=[pltpu.VMEM((12, D, 2, HD), BF16...]
where the time goes in v2:
time: 48.5 us; the launch traced here: 48.4 us
  Pallas kernels  47.1 us (97%)
  local copies, waits for them, and re-layouts  0.71 us (1%)
  between operations  0.65 us (1%)
    pallas_call x1, Pallas kernels, local_layer(): pl.pallas_call(rest_kernel, out_shape=jax.ShapeDtypeStruct((B, D), BF16),...  29.3 us
    pallas_call x1, Pallas kernels, local_layer(): pl.pallas_call(attend_kernel, out_shape=[cache_type, cache_type, jax.Shap...  13 us
    pallas_call x1, Pallas kernels, local_layer(): pl.pallas_call(prepare_kernel, out_shape=[pltpu.VMEM((12, D, 2, HD), BF16...  4.8 us

profile of v2, /device:TPU:0, one launch (start us, length us, event | category | flops | bytes accessed | tf_op | source)
XLA Modules:
  0.0 48.4 jit_solution(13530027010057446328)
XLA Ops:
  0.6 4.8 %prepare.1 = (bf16[12,2048,2,128]{3,2,1,0:T(2,128)(2,1)S(1)}, bf16[128,4096]{1,0:T(8,128)(2,1)S(1)}) custom-call(bf16[64,2048]{1,0:T(8,128)(2,1)} %x_hbm.3, f32[1,2048]{1,0:T(1,128)} %bitcast.15, bf16[2048,12,2,128]{3,2,1,0:T(2,128)(2,1)} %bitcast.10), custom_call_target="tpu_custom_call" | custom-call | tf_op jit(solution)/shard_map/prepare/pallas_call | solution.py:326
  5.4 13.0 %attend.1 = (bf16[2,32,512,128]{3,2,1,0:T(8,128)(2,1)}, bf16[2,32,512,128]{3,2,1,0:T(8,128)(2,1)}, f32[2,2,136,128]{3,2,1,0:T(8,128)S(1)}) custom-call(bf16[128,4096]{1,0:T(8,128)(2,1)S(1)} %get-tuple-element.8.lhs, bf16[12,4096,128]{2,1,0:T(8,128)(2,1)S(1)} %bitcast.9, s32[64]{0:T(128)} %lens_hbm.1, bf16[2,32,512,128]{3,2,1,0:T(8,128)(2,1)} %bitcast.11, ...), custom_call_target="tpu_custom_call" | custom-call | tf_op jit(solution)/shard_map/attend/pallas_call | solution.py:335
  18.4 29.3 %rest.1 = bf16[64,2048]{1,0:T(8,128)(2,1)S(1)} custom-call(f32[2,2,136,128]{3,2,1,0:T(8,128)S(1)} %get-tuple-element.10.o_ref, bf16[64,2048]{1,0:T(8,128)(2,1)} %x_hbm.3, f32[1,2048]{1,0:T(1,128)} %bitcast.14, bf16[1024,2048]{1,0:T(8,128)(2,1)} %bitcast.13, bf16[2048,4096]{1,0:T(8,128)(2,1)} %wu_hbm.1, bf16[4096,2048]{1,0:T(8,128)(2,1)} %wd_hbm.1), custom_call_target="tpu_custom_call" | custom-call | tf_op jit(solution)/shard_map/rest/pallas_call | solution.py:350
  47.7 0.7 %copy.14 = bf16[64,2048]{1,0:T(8,128)(2,1)} copy(bf16[64,2048]{1,0:T(8,128)(2,1)S(1)} %rest.1) | data formatting | bytes 524288

commit v3 on v2

v3 whole, which is shorter than its diff:
```python
import functools

import jax
import jax.numpy as jnp
from jax import lax
from jax.experimental import pallas as pl
from jax.experimental.pallas import tpu as pltpu
from jax.sharding import PartitionSpec as P

LN_EPS = 1e-5
NEG = -1e30
F32 = jnp.float32
BF16 = jnp.bfloat16
MESH = pl.DeviceIdType.MESH

B = 64
D = 2048
NH = 8
HD = 128
T = 64
NQ = 2 * D
CH = 4
CP = 32 // CH
FH = 2048
AHEAD = 4
NUP = 4
NY = 4
NZ = 4


def layer_norm(x_f32, gain):
    mean = jnp.mean(x_f32, axis=-1, keepdims=True)
    centred = x_f32 - mean
    variance = jnp.mean(centred * centred, axis=-1, keepdims=True)
    return centred * lax.rsqrt(variance + LN_EPS) * gain


def prepare_kernel(x_hbm, g_hbm, w_hbm, w_out, lhs, x_buf, g_buf, small_sem, w_sem):
    small = [pltpu.make_async_copy(x_hbm, x_buf, small_sem.at[0]),
             pltpu.make_async_copy(g_hbm, g_buf, small_sem.at[1])]
    w_copy = [pltpu.make_async_copy(w_hbm.at[:, i], w_out.at[i], w_sem.at[i]) for i in range(12)]
    for c in small + w_copy:
        c.start()
    for c in small:
        c.wait()
    normed = layer_norm(x_buf[...].astype(F32), g_buf[...]).astype(BF16)
    spread = (lax.broadcasted_iota(jnp.int32, (128, 256), 1) // 2
              == lax.broadcasted_iota(jnp.int32, (128, 256), 0)).astype(BF16)
    odd = lax.broadcasted_iota(jnp.int32, (B, 256), 1) % 2 == 1
    for i in range(D // 128):
        twice = jnp.dot(normed[:, i * 128:(i + 1) * 128], spread, preferred_element_type=F32)
        lhs[0:B, i * 256:(i + 1) * 256] = jnp.where(odd, 0.0, twice).astype(BF16)
        lhs[B:2 * B, i * 256:(i + 1) * 256] = jnp.where(odd, twice, 0.0).astype(BF16)
    for c in w_copy:
        c.wait()


def attend_kernel(lhs, w_ref, lens_hbm, k_hbm, v_hbm, k_buf, v_buf, o_ref,
                  lens, q_s, k_s, v_s, small_sem, kin_sem, vin_sem):
    lens_copy = pltpu.make_async_copy(lens_hbm, lens, small_sem)
    lens_copy.start()

    def kv_in(i):
        at = pl.ds(i * 2 * CP, 2 * CP)
        return (pltpu.make_async_copy(k_hbm.at[at], k_buf.at[at], kin_sem.at[i]),
                pltpu.make_async_copy(v_hbm.at[at], v_buf.at[at], vin_sem.at[i]))

    for i in range(AHEAD):
        for c in kv_in(i):
            c.start()

    for i in range(0, 12, 2):
        two = jnp.concatenate([w_ref[i], w_ref[i + 1]], axis=1)
        res = jnp.dot(lhs[...], two, preferred_element_type=F32)
        for n in range(2):
            part, pair = divmod(i + n, 4)
            for parity in range(2):
                h = 2 * pair + parity
                val = res[parity * B:(parity + 1) * B, n * HD:(n + 1) * HD]
                (q_s, k_s, v_s)[part][pl.ds(h, B, stride=NH), :] = val
    lens_copy.wait()

    sp = lax.axis_index("sp")
    tp = lax.axis_index("tp")
    row = lax.broadcasted_iota(jnp.int32, (16, 1), 0)
    slope = jnp.exp2(-8.0 * (tp * NH + row % NH + 1).astype(F32) / (2 * NH))
    col = lax.broadcasted_iota(jnp.int32, (16, NH * T), 1)
    own_head = col % NH == lax.broadcasted_iota(jnp.int32, (16, NH * T), 0) % NH
    pos = jnp.where(own_head, sp * T + col // NH, 1 << 20)
    second = row >= 8
    upper = lax.broadcasted_iota(jnp.int32, (16, HD), 0) >= 8
    lane = lax.broadcasted_iota(jnp.int32, (16, HD), 1)

    def insert(buf, new, b):
        slot = lens[b] - sp * T
        held = jnp.logical_and(slot >= 0, slot < T)
        at = jnp.clip(slot, 0, T - 1)
        rows = pl.ds(pl.multiple_of((at // 2) * 16, 16), 16)
        fresh = new[pl.ds(pl.multiple_of(b * NH, NH), NH), :]
        fresh = jnp.concatenate([fresh, fresh], axis=0)
        keep = jnp.where(held, at % 2, 2)
        old = buf[b, rows, :].astype(F32)
        buf[b, rows, :] = jnp.where(upper.astype(jnp.int32) == keep, fresh, old).astype(BF16)

    def chunk(step, stats):
        for c in kv_in(step):
            c.wait()

        @pl.when(step + AHEAD < CH)
        def _():
            for c in kv_in(step + AHEAD):
                c.start()

        for n in range(2 * CP):
            insert(k_buf, k_s, step * 2 * CP + n)
            insert(v_buf, v_s, step * 2 * CP + n)
        scores = []
        for n in range(CP):
            j = step * CP + n
            q = q_s[pl.ds(pl.multiple_of(j * 16, 16), 16), :]
            q2 = jnp.concatenate([jnp.where(upper, 0.0, q), jnp.where(upper, q, 0.0)], axis=1).astype(BF16)
            k2 = jnp.concatenate([k_buf[2 * j], k_buf[2 * j + 1]], axis=1)
            scores.append(lax.dot_general(q2, k2, (((1,), (1,)), ((), ())), preferred_element_type=F32))
        weights = []
        for n in range(CP):
            j = step * CP + n
            length = jnp.where(second, lens[2 * j + 1], lens[2 * j])
            valid = pos <= length
            s = scores[n] * HD ** -0.5 - slope * (length - pos).astype(F32)
            s = jnp.where(valid, s, NEG)
            top = jnp.max(s, axis=1, keepdims=True)
            p = jnp.where(valid, jnp.exp(s - top), 0.0)
            total = jnp.sum(p, axis=1, keepdims=True)
            weights.append(p.astype(BF16))
            stats = jnp.where(lane == j, top, jnp.where(lane == 64 + j, total, stats))
        for n in range(CP):
            j = step * CP + n
            v2 = jnp.concatenate([v_buf[2 * j], v_buf[2 * j + 1]], axis=1)
            o = jnp.dot(weights[n], v2, preferred_element_type=F32)
            at = pl.multiple_of((j % 8) * 16, 16)
            o_ref[j // 8, pl.ds(at, 8), :] = o[0:8, :HD]
            o_ref[j // 8, pl.ds(at + 8, 8), :] = o[8:16, HD:]
        return stats

    stats = lax.fori_loop(0, CH, chunk, jnp.zeros((16, HD), F32))
    for i in range(4):
        o_ref[i, 128:144, :] = stats


def write_kernel(k_buf, v_buf, ko_hbm, vo_hbm, k_sem, v_sem):
    copies = []
    for i in range(4):
        at = pl.ds(i * (B // 4), B // 4)
        copies.append(pltpu.make_async_copy(k_buf.at[at], ko_hbm.at[at], k_sem.at[i]))
        copies.append(pltpu.make_async_copy(v_buf.at[at], vo_hbm.at[at], v_sem.at[i]))
    for c in copies:
        c.start()
    for c in copies:
        c.wait()


def rest_kernel(o0, o1, o2, o3, wo_ref, x_hbm, g_hbm, wu_hbm, wd_hbm, out_ref,
                x_buf, g_buf, wu_buf, wd_buf, att, y_send, y_recv, r_buf, r_recv, n_send, n_recv,
                hid, h_send, h_recv, z_send, z_recv, f_send, f_recv,
                in_sem, wu_sem, wd_sem, y_ss, y_rs, r_ss, r_rs, n_ss, n_rs, h_ss, h_rs, z_ss, z_rs, f_ss, f_rs):
    sp = lax.axis_index("sp")
    tp = lax.axis_index("tp")
    x = sp // 2
    c = sp % 2
    core = {"sp": x * 2 + (1 - c)}
    flip = {"sp": (1 - x) * 2 + c}
    other_tp = {"tp": 1 - tp}
    half = D // 2
    yw = D // NY
    fw = FH // NUP
    zw = half // NZ

    def remote(src, dst, ss, rs, dev):
        return pltpu.make_async_remote_copy(src_ref=src, dst_ref=dst, send_sem=ss, recv_sem=rs, device_id=dev,
                                            device_id_type=MESH)

    barrier = pltpu.get_barrier_semaphore()
    for dev in (core, flip, other_tp):
        pl.semaphore_signal(barrier, inc=1, device_id=dev, device_id_type=MESH)

    in_copy = [pltpu.make_async_copy(g_hbm, g_buf, in_sem.at[0]),
               pltpu.make_async_copy(x_hbm.at[pl.ds(pl.multiple_of(sp * 16, 16), 16)], x_buf, in_sem.at[1])]
    wu_copy = [pltpu.make_async_copy(wu_hbm.at[:, pl.ds(pl.multiple_of(c * FH + k * fw, fw), fw)],
                                     wu_buf.at[k], wu_sem.at[k]) for k in range(NUP)]
    wd_copy = [pltpu.make_async_copy(wd_hbm.at[pl.ds(pl.multiple_of((c if n == 0 else 1 - c) * FH, FH), FH),
                                               pl.ds(pl.multiple_of(c * half, half), half)],
                                     wd_buf.at[n], wd_sem.at[n]) for n in range(2)]
    for cp in in_copy + wu_copy:
        cp.start()

    parts = [o0, o1, o2, o3]
    shift = lax.rem(HD - 8 * sp, HD)
    tops = [pltpu.roll(p[128:144, :], shift, 1) for p in parts]
    sums = [pltpu.roll(t, 64, 1) for t in tops]
    top = functools.reduce(jnp.maximum, tops)
    scale = [jnp.exp(t - top) for t in tops]
    total = functools.reduce(jnp.add, [a * s for a, s in zip(scale, sums)])
    scale = [a / total for a in scale]
    for j in range(8):
        acc = None
        for a, p in zip(scale, parts):
            term = p[j * 16:(j + 1) * 16, :] * a[:, j:j + 1]
            acc = term if acc is None else acc + term
        att[j * 16:(j + 1) * 16, :] = acc
    attended = jnp.concatenate([att[pl.ds(h, 16, stride=NH), :] for h in range(NH)], axis=1).astype(BF16)

    pl.semaphore_wait(barrier, 3)
    y_copy = []
    for k in range(NY):
        y_send[k] = jnp.dot(attended, wo_ref[:, k * yw:(k + 1) * yw], preferred_element_type=F32)
        y_copy.append(remote(y_send.at[k], y_recv.at[k], y_ss.at[k], y_rs.at[k], other_tp))
        y_copy[k].start()
    for cp in wd_copy:
        cp.start()
    for cp in in_copy:
        cp.wait()
    for k in range(NY):
        y_copy[k].wait()
        r_buf[k // (NY // 2), :, (k % (NY // 2)) * yw:(k % (NY // 2) + 1) * yw] = \
            x_buf[:, k * yw:(k + 1) * yw].astype(F32) + (y_send[k] + y_recv[k])
    normed = layer_norm(jnp.concatenate([r_buf[0], r_buf[1]], axis=1), g_buf[...]).astype(BF16)
    n_send[...] = normed.astype(F32)
    n_copy = remote(n_send, n_recv, n_ss, n_rs, core)
    n_copy.start()
    r_copy = remote(r_buf.at[1 - c], r_recv, r_ss, r_rs, core)
    r_copy.start()
    n_copy.wait()
    both = jnp.concatenate([normed, n_recv[...].astype(BF16)], axis=0)

    h_copy = []
    for k in range(NUP):
        wu_copy[k].wait()
        u = jnp.dot(both, wu_buf[k], preferred_element_type=F32)
        act = (0.5 * u * (1.0 + lax.erf(u * 0.5 ** 0.5))).astype(BF16)
        hid[:, k * fw:(k + 1) * fw] = act
        h_send[k] = act.astype(F32)
        h_copy.append(remote(h_send.at[k], h_recv.at[k], h_ss.at[k], h_rs.at[k], core))
        h_copy[k].start()
    wd_copy[0].wait()
    mine = [jnp.dot(hid[...], wd_buf[0, :, k * zw:(k + 1) * zw], preferred_element_type=F32) for k in range(NZ)]
    wd_copy[1].wait()
    theirs = []
    for k in range(NUP):
        h_copy[k].wait()
        theirs.append(jnp.concatenate([h_recv[k, 16:32, :], h_recv[k, 0:16, :]], axis=0).astype(BF16))
    theirs = jnp.concatenate(theirs, axis=1)
    z_copy = []
    for k in range(NZ):
        z_send[k] = mine[k] + jnp.dot(theirs, wd_buf[1, :, k * zw:(k + 1) * zw], preferred_element_type=F32)
        z_copy.append(remote(z_send.at[k], z_recv.at[k], z_ss.at[k], z_rs.at[k], other_tp))
        z_copy[k].start()

    def put(block, first, second, cc, k):
        for n, where in enumerate((first, second)):
            out_ref[pl.ds(pl.multiple_of(where * 16, 16), 16),
                    pl.ds(pl.multiple_of(cc * half + k * zw, zw), zw)] = block[n * 16:(n + 1) * 16].astype(BF16)

    sp_core = x * 2 + (1 - c)
    sp_flip = (1 - x) * 2 + c
    sp_diag = (1 - x) * 2 + (1 - c)
    r_copy.wait()
    near, far, fwd = [], [], []
    for k in range(NZ):
        z_copy[k].wait()
        res = jnp.concatenate([r_buf[c, :, k * zw:(k + 1) * zw], r_recv[:, k * zw:(k + 1) * zw]], axis=0)
        val = res + (z_send[k] + z_recv[k])
        f_send[k] = val
        far.append(remote(f_send.at[k], f_recv.at[1, k], f_ss.at[1, k], f_rs.at[1, k], flip))
        far[k].start()
        near.append(remote(f_send.at[k], f_recv.at[0, k], f_ss.at[0, k], f_rs.at[0, k], core))
        near[k].start()
        put(val, sp, sp_core, c, k)
    for k in range(NZ):
        far[k].wait()
        fwd.append(remote(f_recv.at[1, k], f_recv.at[2, k], f_ss.at[2, k], f_rs.at[2, k], core))
        fwd[k].start()
        put(f_recv[1, k], sp_flip, sp_diag, c, k)
        near[k].wait()
        put(f_recv[0, k], sp_core, sp, 1 - c, k)
    for k in range(NZ):
        fwd[k].wait()
        put(f_recv[2, k], sp_diag, sp_flip, 1 - c, k)


def solution(mesh):
    def hbm(a):
        return pltpu.with_memory_space_constraint(a, pltpu.HBM)

    in_hbm = pl.BlockSpec(memory_space=pltpu.HBM)
    in_vmem = pl.BlockSpec(memory_space=pltpu.VMEM)
    dma = pltpu.SemaphoreType.DMA

    def local_layer(x_in, seq_lens, k_cache, v_cache, ln1_gain, w_qkv, w_out, ln2_gain, w_up, w_down):
        caches = [hbm(a.reshape(B, T * NH, HD)) for a in (k_cache, v_cache)]
        sp = lax.axis_index("sp")
        w_split, lhs = pl.pallas_call(
            prepare_kernel,
            out_shape=[pltpu.VMEM((12, D, 2, HD), BF16), pltpu.VMEM((2 * B, NQ), BF16)],
            in_specs=[in_hbm] * 3,
            out_specs=[in_vmem, in_vmem],
            scratch_shapes=[pltpu.VMEM((B, D), BF16), pltpu.VMEM((1, D), F32), dma((2,)), dma((12,))],
            compiler_params=pltpu.CompilerParams(vmem_limit_bytes=16 * 1024 * 1024),
            name="prepare",
        )(hbm(x_in), hbm(ln1_gain.reshape(1, D)), hbm(w_qkv.reshape(D, 12, 2, HD)))
        cache_shape = (B, T * NH, HD)
        k_upd, v_upd, parts = pl.pallas_call(
            attend_kernel,
            out_shape=[pltpu.VMEM(cache_shape, BF16), pltpu.VMEM(cache_shape, BF16),
                       jax.ShapeDtypeStruct((4, 144, HD), F32)],
            in_specs=[in_vmem] * 2 + [in_hbm] * 3,
            out_specs=[in_vmem] * 3,
            scratch_shapes=[
                pltpu.SMEM((B,), jnp.int32),
                pltpu.VMEM((B * NH, HD), F32), pltpu.VMEM((B * NH, HD), F32), pltpu.VMEM((B * NH, HD), F32),
                dma, dma((CH,)), dma((CH,)),
            ],
            compiler_params=pltpu.CompilerParams(vmem_limit_bytes=8 * 1024 * 1024),
            name="attend",
        )(lhs, w_split.reshape(12, NQ, HD), hbm(seq_lens), *caches)
        pieces = [lax.dynamic_index_in_dim(parts, (sp + rel) % 4, 0, keepdims=False) for rel in range(4)]
        moved = [lax.ppermute(pieces[rel], "sp", [(i, (i + rel) % 4) for i in range(4)]) for rel in (1, 2, 3)]
        k_next, v_next = pl.pallas_call(
            write_kernel,
            out_shape=[jax.ShapeDtypeStruct(cache_shape, BF16)] * 2,
            in_specs=[in_vmem] * 2,
            out_specs=[in_hbm] * 2,
            scratch_shapes=[dma((4,)), dma((4,))],
            compiler_params=pltpu.CompilerParams(vmem_limit_bytes=8 * 1024 * 1024),
            cost_estimate=pl.CostEstimate(flops=6 * 10 ** 9, bytes_accessed=16 << 20, transcendentals=0),
            name="write",
        )(k_upd, v_upd)
        x_out = pl.pallas_call(
            rest_kernel,
            out_shape=jax.ShapeDtypeStruct((B, D), BF16),
            in_specs=[in_vmem] * 5 + [in_hbm] * 4,
            out_specs=in_vmem,
            scratch_shapes=[
                pltpu.VMEM((16, D), BF16), pltpu.VMEM((1, D), F32),
                pltpu.VMEM((NUP, D, FH // NUP), BF16),
                pltpu.VMEM((2, FH, D // 2), BF16),
                pltpu.VMEM((128, HD), F32),
                pltpu.VMEM((NY, 16, D // NY), F32), pltpu.VMEM((NY, 16, D // NY), F32),
                pltpu.VMEM((2, 16, D // 2), F32), pltpu.VMEM((16, D // 2), F32),
                pltpu.VMEM((16, D), F32), pltpu.VMEM((16, D), F32),
                pltpu.VMEM((32, FH), BF16),
                pltpu.VMEM((NUP, 32, FH // NUP), F32), pltpu.VMEM((NUP, 32, FH // NUP), F32),
                pltpu.VMEM((NZ, 32, D // 2 // NZ), F32), pltpu.VMEM((NZ, 32, D // 2 // NZ), F32),
                pltpu.VMEM((NZ, 32, D // 2 // NZ), F32), pltpu.VMEM((3, NZ, 32, D // 2 // NZ), F32),
                dma((2,)), dma((NUP,)), dma((2,)),
                dma((NY,)), dma((NY,)), dma, dma, dma, dma, dma((NUP,)), dma((NUP,)),
                dma((NZ,)), dma((NZ,)), dma((3, NZ)), dma((3, NZ)),
            ],
            compiler_params=pltpu.CompilerParams(vmem_limit_bytes=32 * 1024 * 1024, collective_id=0,
                                                 has_side_effects=True),
            cost_estimate=pl.CostEstimate(flops=10 ** 10, bytes_accessed=20 << 20, transcendentals=0),
            name="rest",
        )(pieces[0], *moved, w_out.reshape(NH * HD, D), hbm(x_in), hbm(ln2_gain.reshape(1, D)), hbm(w_up), hbm(w_down))
        return x_out, k_next.reshape(k_cache.shape), v_next.reshape(v_cache.shape)

    cache_spec = P("dp", "sp", "tp", None)
    in_specs = (P("dp", None), P("dp"), cache_spec, cache_spec, P(None), P(None, None, "tp", None), P("tp", None, None), P(None), P(None, "tp"), P("tp", None))
    out_specs = (P("dp", None), cache_spec, cache_spec)
    return jax.shard_map(local_layer, mesh=mesh, in_specs=in_specs, out_specs=out_specs, check_vma=False)
```

time: 48.5 us -> 45.3 us (0.934)
  Pallas kernels: 47.1 us -> 40.1 us
  starting transfers between devices: 0 us -> 3.59 us
    pallas_call x1, Pallas kernels: 29.3 us -> 21.3 us  [local_layer(): pl.pallas_call(rest_kernel, out_shape=jax.ShapeDtypeStruct((B, D), BF16),...]
    ppermute x0 -> x3, starting transfers between devices: none -> 3.59 us  [local_layer(): lax.ppermute(pieces[rel], 'sp', [(i, (i + rel) % 4) for i in range(4)])]
    pallas_call x1 -> x2, Pallas kernels: 13 us -> 14 us  [the longest x1 7.21 us: local_layer(): pl.pallas_call(attend_kernel, out_shape=[pltpu.VMEM(cache_shape, BF16), p...]
  transfers between devices with their start and end apart: 0 -> 3, of which waited for: 0 -> 0; matrix products, arithmetic and copies ran while one was open for 0% -> 0% of each run, Pallas kernels for 0% -> 15%
where the time goes in v3:
time: 45.3 us; the launch traced here: 45.2 us
  Pallas kernels  40.1 us (89%)
  starting transfers between devices  3.59 us (8%)
  between operations  0.76 us (2%)
  local copies, waits for them, and re-layouts  0.74 us (2%)
    pallas_call x1, Pallas kernels, local_layer(): pl.pallas_call(rest_kernel, out_shape=jax.ShapeDtypeStruct((B, D), BF16),...  21.3 us
    pallas_call x1, Pallas kernels, local_layer(): pl.pallas_call(attend_kernel, out_shape=[pltpu.VMEM(cache_shape, BF16), p...  7.21 us
    pallas_call x1, Pallas kernels, local_layer(): pl.pallas_call(write_kernel, out_shape=[jax.ShapeDtypeStruct(cache_shape,...  6.77 us
    pallas_call x1, Pallas kernels, local_layer(): pl.pallas_call(prepare_kernel, out_shape=[pltpu.VMEM((12, D, 2, HD), BF16...  4.8 us
    ppermute x3, starting transfers between devices, local_layer(): lax.ppermute(pieces[rel], 'sp', [(i, (i + rel) % 4) for i in range(4)])  3.59 us
  transfers between devices with their start and end apart: 3, of which 0 were waited for; matrix products, arithmetic and copies ran while one was open for 0% of the time, Pallas kernels for 15%

profile of v3, /device:TPU:0, one launch (start us, length us, event | category | flops | bytes accessed | tf_op | source)
XLA Modules:
  0.0 45.2 jit_solution(17235241728832804545)
XLA Ops:
  0.7 4.8 %prepare.1 = (bf16[12,2048,2,128]{3,2,1,0:T(2,128)(2,1)S(1)}, bf16[128,4096]{1,0:T(8,128)(2,1)S(1)}) custom-call(bf16[64,2048]{1,0:T(8,128)(2,1)} %x_hbm.3, f32[1,2048]{1,0:T(1,128)} %bitcast.23, bf16[2048,12,2,128]{3,2,1,0:T(2,128)(2,1)} %bitcast.19), custom_call_target="tpu_custom_call" | custom-call | tf_op jit(solution)/shard_map/prepare/pallas_call | solution.py:301
  5.5 7.2 %attend.1 = (bf16[64,512,128]{2,1,0:T(8,128)(2,1)S(1)}, bf16[64,512,128]{2,1,0:T(8,128)(2,1)S(1)}, f32[4,144,128]{2,1,0:T(8,128)S(1)}) custom-call(bf16[128,4096]{1,0:T(8,128)(2,1)S(1)} %get-tuple-element.10.lhs, bf16[12,4096,128]{2,1,0:T(8,128)(2,1)S(1)} %bitcast.17, s32[64]{0:T(128)} %lens_hbm.1, bf16[64,512,128]{2,1,0:T(8,128)(2,1)} %bitcast.20, ...), custom_call_target="tpu_custom_call" | custom-call | tf_op jit(solution)/shard_map/attend/pallas_call | solution.py:311
  12.8 2.8 %collective-permute-start.2 = (f32[144,128]{1,0:T(8,128)S(1)}, f32[144,128]{1,0:T(8,128)S(1)}, u32[]{:S(2)}, u32[]{:S(2)}) collective-permute-start(f32[144,128]{1,0:T(8,128)S(1)} %get-tuple-element.17), channel_id=1, source_target_pairs={{0,3},{1,0},{2,1},{3,2},{4,7},{5,4},{6,5},{7,6}} | collective-permute-start | bytes 221192 | tf_op jit(solution)/shard_map/ppermute | solution.py:326
  15.6 0.6 %collective-permute-start.1 = (f32[144,128]{1,0:T(8,128)S(1)}, f32[144,128]{1,0:T(8,128)S(1)}, u32[]{:S(2)}, u32[]{:S(2)}) collective-permute-start(f32[144,128]{1,0:T(8,128)S(1)} %get-tuple-element.18), channel_id=1, source_target_pairs={{0,2},{1,3},{2,0},{3,1},{4,6},{5,7},{6,4},{7,5}} | collective-permute-start | bytes 221192 | tf_op jit(solution)/shard_map/ppermute | solution.py:326
  16.2 0.2 collective-permute-start
  16.4 0.0 copy-start
  16.4 6.8 %write.1 = (bf16[64,512,128]{2,1,0:T(8,128)(2,1)}, bf16[64,512,128]{2,1,0:T(8,128)(2,1)}) custom-call(bf16[64,512,128]{2,1,0:T(8,128)(2,1)S(1)} %get-tuple-element.13.k_buf, bf16[64,512,128]{2,1,0:T(8,128)(2,1)S(1)} %get-tuple-element.14.v_buf), custom_call_target="tpu_custom_call" | custom-call | flops 6000000000 | bytes 16777216 | tf_op jit(solution)/shard_map/write/pallas_call | solution.py:327
  23.1 0.0 collective-permute-done.2.o3
  23.1 0.0 collective-permute-done.1.o2
  23.2 0.0 collective-permute-done.o1
  23.2 0.0 copy-done
  23.2 21.3 %rest.1 = bf16[64,2048]{1,0:T(8,128)(2,1)S(1)} custom-call(f32[144,128]{1,0:T(8,128)S(1)} %get-tuple-element.20.o0, f32[144,128]{1,0:T(8,128)S(1)} %collective-permute-done.o1, f32[144,128]{1,0:T(8,128)S(1)} %collective-permute-done.1.o2, f32[144,128]{1,0:T(8,128)S(1)} %collective-permute-done.2.o3, bf16[1024,2048]{1,0:T(8,128)(2,1)S(1)} %bitcast.18, ...), custom_call_target="tpu_custom_call" | custom-call | flops 10000000000 | bytes 20971520 | tf_op jit(solution)/shard_map/rest/pallas_call | solution.py:337
  44.5 0.7 %copy.14 = bf16[64,2048]{1,0:T(8,128)(2,1)} copy(bf16[64,2048]{1,0:T(8,128)(2,1)S(1)} %rest.1) | data formatting | bytes 524288
  (1 shorter events, 0.0 us)
Async XLA Ops:
  12.8 10.4 %collective-permute-start.2 = (f32[144,128]{1,0:T(8,128)S(1)}, f32[144,128]{1,0:T(8,128)S(1)}, u32[]{:S(2)}, u32[]{:S(2)}) collective-permute-start(f32[144,128]{1,0:T(8,128)S(1)} %get-tuple-element.17), channel_id=1, source_target_pairs={{0,3},{1,0},{2,1},{3,2},{4,7},{5,4},{6,5},{7,6}} | collective-permute-start | bytes 221192 | tf_op jit(solution)/shard_map/ppermute | solution.py:326
  15.6 7.6 %collective-permute-start.1 = (f32[144,128]{1,0:T(8,128)S(1)}, f32[144,128]{1,0:T(8,128)S(1)}, u32[]{:S(2)}, u32[]{:S(2)}) collective-permute-start(f32[144,128]{1,0:T(8,128)S(1)} %get-tuple-element.18), channel_id=1, source_target_pairs={{0,2},{1,3},{2,0},{3,1},{4,6},{5,7},{6,4},{7,5}} | collective-permute-start | bytes 221192 | tf_op jit(solution)/shard_map/ppermute | solution.py:326
  16.2 7.0 %collective-permute-start = (f32[144,128]{1,0:T(8,128)S(1)}, f32[144,128]{1,0:T(8,128)S(1)}, u32[]{:S(2)}, u32[]{:S(2)}) collective-permute-start(f32[144,128]{1,0:T(8,128)S(1)} %get-tuple-element.19), channel_id=1, source_target_pairs={{0,1},{1,2},{2,3},{3,0},{4,5},{5,6},{6,7},{7,4}} | collective-permute-start | bytes 221192 | tf_op jit(solution)/shard_map/ppermute | solution.py:326
  16.4 6.8 %copy-start = (bf16[8,128,2048]{2,1,0:T(8,128)(2,1)S(1)}, bf16[8,128,2048]{2,1,0:T(8,128)(2,1)}, u32[]{:S(2)}) copy-start(bf16[8,128,2048]{2,1,0:T(8,128)(2,1)} %param.16) | copy-start | bytes 12582916

commit v4 on v3

--- a/solution.py
+++ b/solution.py
@@ -21,9 +21,8 @@
 NQ = 2 * D
 CH = 4
 CP = 32 // CH
-FH = 2048
 AHEAD = 4
-NUP = 4
+NUP = 2
 NY = 4
 NZ = 4
 
@@ -160,36 +159,32 @@
 
 
 def rest_kernel(o0, o1, o2, o3, wo_ref, x_hbm, g_hbm, wu_hbm, wd_hbm, out_ref,
-                x_buf, g_buf, wu_buf, wd_buf, att, y_send, y_recv, r_buf, r_recv, n_send, n_recv,
-                hid, h_send, h_recv, z_send, z_recv, f_send, f_recv,
-                in_sem, wu_sem, wd_sem, y_ss, y_rs, r_ss, r_rs, n_ss, n_rs, h_ss, h_rs, z_ss, z_rs, f_ss, f_rs):
+                x_buf, g_buf, wu_buf, wd_buf, att, y_send, y_recv, r_buf, hid, z_send, z_recv, f_send, f_recv,
+                in_sem, wu_sem, wd_sem, y_ss, y_rs, z_ss, z_rs, f_ss, f_rs):
     sp = lax.axis_index("sp")
     tp = lax.axis_index("tp")
     x = sp // 2
     c = sp % 2
-    core = {"sp": x * 2 + (1 - c)}
-    flip = {"sp": (1 - x) * 2 + c}
+    sp_core = x * 2 + (1 - c)
+    sp_flip = (1 - x) * 2 + c
+    sp_diag = (1 - x) * 2 + (1 - c)
     other_tp = {"tp": 1 - tp}
-    half = D // 2
     yw = D // NY
-    fw = FH // NUP
-    zw = half // NZ
+    fw = wu_hbm.shape[1] // NUP
+    zw = D // NZ
 
     def remote(src, dst, ss, rs, dev):
         return pltpu.make_async_remote_copy(src_ref=src, dst_ref=dst, send_sem=ss, recv_sem=rs, device_id=dev,
                                             device_id_type=MESH)
 
     barrier = pltpu.get_barrier_semaphore()
-    for dev in (core, flip, other_tp):
+    for dev in ({"sp": sp_core}, {"sp": sp_flip}, {"sp": sp_diag}, other_tp):
         pl.semaphore_signal(barrier, inc=1, device_id=dev, device_id_type=MESH)
 
     in_copy = [pltpu.make_async_copy(g_hbm, g_buf, in_sem.at[0]),
                pltpu.make_async_copy(x_hbm.at[pl.ds(pl.multiple_of(sp * 16, 16), 16)], x_buf, in_sem.at[1])]
-    wu_copy = [pltpu.make_async_copy(wu_hbm.at[:, pl.ds(pl.multiple_of(c * FH + k * fw, fw), fw)],
-                                     wu_buf.at[k], wu_sem.at[k]) for k in range(NUP)]
-    wd_copy = [pltpu.make_async_copy(wd_hbm.at[pl.ds(pl.multiple_of((c if n == 0 else 1 - c) * FH, FH), FH),
-                                               pl.ds(pl.multiple_of(c * half, half), half)],
-                                     wd_buf.at[n], wd_sem.at[n]) for n in range(2)]
+    wu_copy = [pltpu.make_async_copy(wu_hbm.at[:, k * fw:(k + 1) * fw], wu_buf.at[k], wu_sem.at[k]) for k in range(NUP)]
+    wd_copy = [pltpu.make_async_copy(wd_hbm.at[:, k * zw:(k + 1) * zw], wd_buf.at[k], wd_sem.at[k]) for k in range(NZ)]
     for cp in in_copy + wu_copy:
         cp.start()
 
@@ -209,82 +204,66 @@
         att[j * 16:(j + 1) * 16, :] = acc
     attended = jnp.concatenate([att[pl.ds(h, 16, stride=NH), :] for h in range(NH)], axis=1).astype(BF16)
 
-    pl.semaphore_wait(barrier, 3)
+    pl.semaphore_wait(barrier, 4)
     y_copy = []
     for k in range(NY):
         y_send[k] = jnp.dot(attended, wo_ref[:, k * yw:(k + 1) * yw], preferred_element_type=F32)
         y_copy.append(remote(y_send.at[k], y_recv.at[k], y_ss.at[k], y_rs.at[k], other_tp))
         y_copy[k].start()
-    for cp in wd_copy:
-        cp.start()
     for cp in in_copy:
         cp.wait()
     for k in range(NY):
         y_copy[k].wait()
-        r_buf[k // (NY // 2), :, (k % (NY // 2)) * yw:(k % (NY // 2) + 1) * yw] = \
-            x_buf[:, k * yw:(k + 1) * yw].astype(F32) + (y_send[k] + y_recv[k])
-    normed = layer_norm(jnp.concatenate([r_buf[0], r_buf[1]], axis=1), g_buf[...]).astype(BF16)
-    n_send[...] = normed.astype(F32)
-    n_copy = remote(n_send, n_recv, n_ss, n_rs, core)
-    n_copy.start()
-    r_copy = remote(r_buf.at[1 - c], r_recv, r_ss, r_rs, core)
-    r_copy.start()
-    n_copy.wait()
-    both = jnp.concatenate([normed, n_recv[...].astype(BF16)], axis=0)
-
-    h_copy = []
+        if k == 0:
+            for cp in wd_copy:
+                cp.start()
+        cols = slice(k * yw, (k + 1) * yw)
+        r_buf[:, cols] = x_buf[:, cols].astype(F32) + (y_send[k] + y_recv[k])
+    normed = layer_norm(r_buf[...], g_buf[...]).astype(BF16)
+
     for k in range(NUP):
         wu_copy[k].wait()
-        u = jnp.dot(both, wu_buf[k], preferred_element_type=F32)
-        act = (0.5 * u * (1.0 + lax.erf(u * 0.5 ** 0.5))).astype(BF16)
-        hid[:, k * fw:(k + 1) * fw] = act
-        h_send[k] = act.astype(F32)
-        h_copy.append(remote(h_send.at[k], h_recv.at[k], h_ss.at[k], h_rs.at[k], core))
-        h_copy[k].start()
-    wd_copy[0].wait()
-    mine = [jnp.dot(hid[...], wd_buf[0, :, k * zw:(k + 1) * zw], preferred_element_type=F32) for k in range(NZ)]
-    wd_copy[1].wait()
-    theirs = []
-    for k in range(NUP):
-        h_copy[k].wait()
-        theirs.append(jnp.concatenate([h_recv[k, 16:32, :], h_recv[k, 0:16, :]], axis=0).astype(BF16))
-    theirs = jnp.concatenate(theirs, axis=1)
+        u = jnp.dot(normed, wu_buf[k], preferred_element_type=F32)
+        hid[:, k * fw:(k + 1) * fw] = (0.5 * u * (1.0 + lax.erf(u * 0.5 ** 0.5))).astype(BF16)
     z_copy = []
     for k in range(NZ):
-        z_send[k] = mine[k] + jnp.dot(theirs, wd_buf[1, :, k * zw:(k + 1) * zw], preferred_element_type=F32)
+        wd_copy[k].wait()
+        z_send[k] = jnp.dot(hid[...], wd_buf[k], preferred_element_type=F32)
         z_copy.append(remote(z_send.at[k], z_recv.at[k], z_ss.at[k], z_rs.at[k], other_tp))
         z_copy[k].start()
 
-    def put(block, first, second, cc, k):
-        for n, where in enumerate((first, second)):
-            out_ref[pl.ds(pl.multiple_of(where * 16, 16), 16),
-                    pl.ds(pl.multiple_of(cc * half + k * zw, zw), zw)] = block[n * 16:(n + 1) * 16].astype(BF16)
-
-    sp_core = x * 2 + (1 - c)
-    sp_flip = (1 - x) * 2 + c
-    sp_diag = (1 - x) * 2 + (1 - c)
-    r_copy.wait()
-    near, far, fwd = [], [], []
+    def put(block, where, k):
+        out_ref[pl.ds(pl.multiple_of(where * 16, 16), 16), k * zw:(k + 1) * zw] = block.astype(BF16)
+
+    near, far, diag = [], [], []
+
+    def arrived(k):
+        far[k].wait()
+        if k < NZ - 1:
+            diag.append(remote(f_recv.at[1, k], f_recv.at[2, k], f_ss.at[2, k], f_rs.at[2, k], {"sp": sp_core}))
+            diag[k].start()
+        put(f_recv[1, k], sp_flip, k)
+
     for k in range(NZ):
         z_copy[k].wait()
-        res = jnp.concatenate([r_buf[c, :, k * zw:(k + 1) * zw], r_recv[:, k * zw:(k + 1) * zw]], axis=0)
-        val = res + (z_send[k] + z_recv[k])
+        val = r_buf[:, k * zw:(k + 1) * zw] + (z_send[k] + z_recv[k])
         f_send[k] = val
-        far.append(remote(f_send.at[k], f_recv.at[1, k], f_ss.at[1, k], f_rs.at[1, k], flip))
+        far.append(remote(f_send.at[k], f_recv.at[1, k], f_ss.at[1, k], f_rs.at[1, k], {"sp": sp_flip}))
         far[k].start()
-        near.append(remote(f_send.at[k], f_recv.at[0, k], f_ss.at[0, k], f_rs.at[0, k], core))
+        if k == NZ - 1:
+            last = remote(f_send.at[k], f_recv.at[2, k], f_ss.at[2, k], f_rs.at[2, k], {"sp": sp_diag})
+            last.start()
+        near.append(remote(f_send.at[k], f_recv.at[0, k], f_ss.at[0, k], f_rs.at[0, k], {"sp": sp_core}))
         near[k].start()
-        put(val, sp, sp_core, c, k)
+        put(val, sp, k)
     for k in range(NZ):
-        far[k].wait()
-        fwd.append(remote(f_recv.at[1, k], f_recv.at[2, k], f_ss.at[2, k], f_rs.at[2, k], core))
-        fwd[k].start()
-        put(f_recv[1, k], sp_flip, sp_diag, c, k)
         near[k].wait()
-        put(f_recv[0, k], sp_core, sp, 1 - c, k)
+        put(f_recv[0, k], sp_core, k)
+        arrived(k)
+    diag.append(last)
     for k in range(NZ):
-        fwd[k].wait()
-        put(f_recv[2, k], sp_diag, sp_flip, 1 - c, k)
+        diag[k].wait()
+        put(f_recv[2, k], sp_diag, k)
 
 
 def solution(mesh):
@@ -308,6 +287,7 @@
             name="prepare",
         )(hbm(x_in), hbm(ln1_gain.reshape(1, D)), hbm(w_qkv.reshape(D, 12, 2, HD)))
         cache_shape = (B, T * NH, HD)
+        ff = w_up.shape[1]
         k_upd, v_upd, parts = pl.pallas_call(
             attend_kernel,
             out_shape=[pltpu.VMEM(cache_shape, BF16), pltpu.VMEM(cache_shape, BF16),
@@ -341,21 +321,16 @@
             out_specs=in_vmem,
             scratch_shapes=[
                 pltpu.VMEM((16, D), BF16), pltpu.VMEM((1, D), F32),
-                pltpu.VMEM((NUP, D, FH // NUP), BF16),
-                pltpu.VMEM((2, FH, D // 2), BF16),
+                pltpu.VMEM((NUP, D, ff // NUP), BF16), pltpu.VMEM((NZ, ff, D // NZ), BF16),
                 pltpu.VMEM((128, HD), F32),
                 pltpu.VMEM((NY, 16, D // NY), F32), pltpu.VMEM((NY, 16, D // NY), F32),
-                pltpu.VMEM((2, 16, D // 2), F32), pltpu.VMEM((16, D // 2), F32),
-                pltpu.VMEM((16, D), F32), pltpu.VMEM((16, D), F32),
-                pltpu.VMEM((32, FH), BF16),
-                pltpu.VMEM((NUP, 32, FH // NUP), F32), pltpu.VMEM((NUP, 32, FH // NUP), F32),
-                pltpu.VMEM((NZ, 32, D // 2 // NZ), F32), pltpu.VMEM((NZ, 32, D // 2 // NZ), F32),
-                pltpu.VMEM((NZ, 32, D // 2 // NZ), F32), pltpu.VMEM((3, NZ, 32, D // 2 // NZ), F32),
-                dma((2,)), dma((NUP,)), dma((2,)),
-                dma((NY,)), dma((NY,)), dma, dma, dma, dma, dma((NUP,)), dma((NUP,)),
-                dma((NZ,)), dma((NZ,)), dma((3, NZ)), dma((3, NZ)),
+                pltpu.VMEM((16, D), F32), pltpu.VMEM((16, ff), BF16),
+                pltpu.VMEM((NZ, 16, D // NZ), F32), pltpu.VMEM((NZ, 16, D // NZ), F32),
+                pltpu.VMEM((NZ, 16, D // NZ), F32), pltpu.VMEM((3, NZ, 16, D // NZ), F32),
+                dma((2,)), dma((NUP,)), dma((NZ,)),
+                dma((NY,)), dma((NY,)), dma((NZ,)), dma((NZ,)), dma((3, NZ)), dma((3, NZ)),
             ],
-            compiler_params=pltpu.CompilerParams(vmem_limit_bytes=32 * 1024 * 1024, collective_id=0,
+            compiler_params=pltpu.CompilerParams(vmem_limit_bytes=40 * 1024 * 1024, collective_id=0,
                                                  has_side_effects=True),
             cost_estimate=pl.CostEstimate(flops=10 ** 10, bytes_accessed=20 << 20, transcendentals=0),
             name="rest",

time: 45.3 us -> 43.1 us (0.951)
  Pallas kernels: 40.1 us -> 37.9 us
    pallas_call x1, Pallas kernels: 21.3 us -> 19.1 us  [local_layer(): pl.pallas_call(rest_kernel, out_shape=jax.ShapeDtypeStruct((B, D), BF16),...]
  transfers between devices with their start and end apart: 3 -> 3, of which waited for: 0 -> 0; matrix products, arithmetic and copies ran while one was open for 0% -> 0% of each run, Pallas kernels for 15% -> 16%
where the time goes in v4:
time: 43.1 us; the launch traced here: 43 us
  Pallas kernels  37.9 us (88%)
  starting transfers between devices  3.59 us (8%)
  between operations  0.76 us (2%)
  local copies, waits for them, and re-layouts  0.74 us (2%)
    pallas_call x1, Pallas kernels, local_layer(): pl.pallas_call(rest_kernel, out_shape=jax.ShapeDtypeStruct((B, D), BF16),...  19.1 us
    pallas_call x1, Pallas kernels, local_layer(): pl.pallas_call(attend_kernel, out_shape=[pltpu.VMEM(cache_shape, BF16), p...  7.22 us
    pallas_call x1, Pallas kernels, local_layer(): pl.pallas_call(write_kernel, out_shape=[jax.ShapeDtypeStruct(cache_shape,...  6.77 us
    pallas_call x1, Pallas kernels, local_layer(): pl.pallas_call(prepare_kernel, out_shape=[pltpu.VMEM((12, D, 2, HD), BF16...  4.8 us
    ppermute x3, starting transfers between devices, local_layer(): lax.ppermute(pieces[rel], 'sp', [(i, (i + rel) % 4) for i in range(4)])  3.59 us
  transfers between devices with their start and end apart: 3, of which 0 were waited for; matrix products, arithmetic and copies ran while one was open for 0% of the time, Pallas kernels for 16%

profile of v4, /device:TPU:0, one launch (start us, length us, event | category | flops | bytes accessed | tf_op | source)
XLA Modules:
  0.0 43.0 jit_solution(1133692807096306451)
XLA Ops:
  0.7 4.8 %prepare.1 = (bf16[12,2048,2,128]{3,2,1,0:T(2,128)(2,1)S(1)}, bf16[128,4096]{1,0:T(8,128)(2,1)S(1)}) custom-call(bf16[64,2048]{1,0:T(8,128)(2,1)} %x_hbm.3, f32[1,2048]{1,0:T(1,128)} %bitcast.23, bf16[2048,12,2,128]{3,2,1,0:T(2,128)(2,1)} %bitcast.19), custom_call_target="tpu_custom_call" | custom-call | tf_op jit(solution)/shard_map/prepare/pallas_call | solution.py:280
  5.5 7.2 %attend.1 = (bf16[64,512,128]{2,1,0:T(8,128)(2,1)S(1)}, bf16[64,512,128]{2,1,0:T(8,128)(2,1)S(1)}, f32[4,144,128]{2,1,0:T(8,128)S(1)}) custom-call(bf16[128,4096]{1,0:T(8,128)(2,1)S(1)} %get-tuple-element.10.lhs, bf16[12,4096,128]{2,1,0:T(8,128)(2,1)S(1)} %bitcast.17, s32[64]{0:T(128)} %lens_hbm.1, bf16[64,512,128]{2,1,0:T(8,128)(2,1)} %bitcast.20, ...), custom_call_target="tpu_custom_call" | custom-call | tf_op jit(solution)/shard_map/attend/pallas_call | solution.py:291
  12.8 2.8 %collective-permute-start.2 = (f32[144,128]{1,0:T(8,128)S(1)}, f32[144,128]{1,0:T(8,128)S(1)}, u32[]{:S(2)}, u32[]{:S(2)}) collective-permute-start(f32[144,128]{1,0:T(8,128)S(1)} %get-tuple-element.17), channel_id=1, source_target_pairs={{0,3},{1,0},{2,1},{3,2},{4,7},{5,4},{6,5},{7,6}} | collective-permute-start | bytes 221192 | tf_op jit(solution)/shard_map/ppermute | solution.py:306
  15.6 0.6 %collective-permute-start.1 = (f32[144,128]{1,0:T(8,128)S(1)}, f32[144,128]{1,0:T(8,128)S(1)}, u32[]{:S(2)}, u32[]{:S(2)}) collective-permute-start(f32[144,128]{1,0:T(8,128)S(1)} %get-tuple-element.18), channel_id=1, source_target_pairs={{0,2},{1,3},{2,0},{3,1},{4,6},{5,7},{6,4},{7,5}} | collective-permute-start | bytes 221192 | tf_op jit(solution)/shard_map/ppermute | solution.py:306
  16.2 0.2 collective-permute-start
  16.4 0.0 copy-start
  16.4 6.8 %write.1 = (bf16[64,512,128]{2,1,0:T(8,128)(2,1)}, bf16[64,512,128]{2,1,0:T(8,128)(2,1)}) custom-call(bf16[64,512,128]{2,1,0:T(8,128)(2,1)S(1)} %get-tuple-element.13.k_buf, bf16[64,512,128]{2,1,0:T(8,128)(2,1)S(1)} %get-tuple-element.14.v_buf), custom_call_target="tpu_custom_call" | custom-call | flops 6000000000 | bytes 16777216 | tf_op jit(solution)/shard_map/write/pallas_call | solution.py:307
  23.1 0.0 collective-permute-done.2.o3
  23.1 0.0 collective-permute-done.1.o2
  23.2 0.0 collective-permute-done.o1
  23.2 0.0 copy-done
  23.2 19.1 %rest.1 = bf16[64,2048]{1,0:T(8,128)(2,1)S(1)} custom-call(f32[144,128]{1,0:T(8,128)S(1)} %get-tuple-element.20.o0, f32[144,128]{1,0:T(8,128)S(1)} %collective-permute-done.o1, f32[144,128]{1,0:T(8,128)S(1)} %collective-permute-done.1.o2, f32[144,128]{1,0:T(8,128)S(1)} %collective-permute-done.2.o3, bf16[1024,2048]{1,0:T(8,128)(2,1)S(1)} %bitcast.18, ...), custom_call_target="tpu_custom_call" | custom-call | flops 10000000000 | bytes 20971520 | tf_op jit(solution)/shard_map/rest/pallas_call | solution.py:317
  42.3 0.7 %copy.14 = bf16[64,2048]{1,0:T(8,128)(2,1)} copy(bf16[64,2048]{1,0:T(8,128)(2,1)S(1)} %rest.1) | data formatting | bytes 524288
  (1 shorter events, 0.0 us)
Async XLA Ops:
  12.8 10.4 %collective-permute-start.2 = (f32[144,128]{1,0:T(8,128)S(1)}, f32[144,128]{1,0:T(8,128)S(1)}, u32[]{:S(2)}, u32[]{:S(2)}) collective-permute-start(f32[144,128]{1,0:T(8,128)S(1)} %get-tuple-element.17), channel_id=1, source_target_pairs={{0,3},{1,0},{2,1},{3,2},{4,7},{5,4},{6,5},{7,6}} | collective-permute-start | bytes 221192 | tf_op jit(solution)/shard_map/ppermute | solution.py:306
  15.6 7.6 %collective-permute-start.1 = (f32[144,128]{1,0:T(8,128)S(1)}, f32[144,128]{1,0:T(8,128)S(1)}, u32[]{:S(2)}, u32[]{:S(2)}) collective-permute-start(f32[144,128]{1,0:T(8,128)S(1)} %get-tuple-element.18), channel_id=1, source_target_pairs={{0,2},{1,3},{2,0},{3,1},{4,6},{5,7},{6,4},{7,5}} | collective-permute-start | bytes 221192 | tf_op jit(solution)/shard_map/ppermute | solution.py:306
  16.2 7.0 %collective-permute-start = (f32[144,128]{1,0:T(8,128)S(1)}, f32[144,128]{1,0:T(8,128)S(1)}, u32[]{:S(2)}, u32[]{:S(2)}) collective-permute-start(f32[144,128]{1,0:T(8,128)S(1)} %get-tuple-element.19), channel_id=1, source_target_pairs={{0,1},{1,2},{2,3},{3,0},{4,5},{5,6},{6,7},{7,4}} | collective-permute-start | bytes 221192 | tf_op jit(solution)/shard_map/ppermute | solution.py:306
  16.4 6.8 %copy-start = (bf16[8,128,2048]{2,1,0:T(8,128)(2,1)S(1)}, bf16[8,128,2048]{2,1,0:T(8,128)(2,1)}, u32[]{:S(2)}) copy-start(bf16[8,128,2048]{2,1,0:T(8,128)(2,1)} %param.16) | copy-start | bytes 12582916

commit v5 on v4

--- a/solution.py
+++ b/solution.py
@@ -22,7 +22,7 @@
 CH = 4
 CP = 32 // CH
 AHEAD = 4
-NUP = 2
+NUP = 1
 NY = 4
 NZ = 4
 

time: 43.1 us -> 43 us (level)
  no operation moved by 1% of the time
where the time goes in v5:
time: 43 us; the launch traced here: 42.9 us
  Pallas kernels  37.8 us (88%)
  starting transfers between devices  3.59 us (8%)
  between operations  0.76 us (2%)
  local copies, waits for them, and re-layouts  0.74 us (2%)
    pallas_call x1, Pallas kernels, local_layer(): pl.pallas_call(rest_kernel, out_shape=jax.ShapeDtypeStruct((B, D), BF16),...  19.1 us
    pallas_call x1, Pallas kernels, local_layer(): pl.pallas_call(attend_kernel, out_shape=[pltpu.VMEM(cache_shape, BF16), p...  7.22 us
    pallas_call x1, Pallas kernels, local_layer(): pl.pallas_call(write_kernel, out_shape=[jax.ShapeDtypeStruct(cache_shape,...  6.77 us
    pallas_call x1, Pallas kernels, local_layer(): pl.pallas_call(prepare_kernel, out_shape=[pltpu.VMEM((12, D, 2, HD), BF16...  4.8 us
    ppermute x3, starting transfers between devices, local_layer(): lax.ppermute(pieces[rel], 'sp', [(i, (i + rel) % 4) for i in range(4)])  3.59 us
  transfers between devices with their start and end apart: 3, of which 0 were waited for; matrix products, arithmetic and copies ran while one was open for 0% of the time, Pallas kernels for 16%

profile of v5, /device:TPU:0, one launch (start us, length us, event | category | flops | bytes accessed | tf_op | source)
XLA Modules:
  0.0 42.9 jit_solution(7925779041942131054)
XLA Ops:
  0.7 4.8 %prepare.1 = (bf16[12,2048,2,128]{3,2,1,0:T(2,128)(2,1)S(1)}, bf16[128,4096]{1,0:T(8,128)(2,1)S(1)}) custom-call(bf16[64,2048]{1,0:T(8,128)(2,1)} %x_hbm.3, f32[1,2048]{1,0:T(1,128)} %bitcast.23, bf16[2048,12,2,128]{3,2,1,0:T(2,128)(2,1)} %bitcast.19), custom_call_target="tpu_custom_call" | custom-call | tf_op jit(solution)/shard_map/prepare/pallas_call | solution.py:280
  5.5 7.2 %attend.1 = (bf16[64,512,128]{2,1,0:T(8,128)(2,1)S(1)}, bf16[64,512,128]{2,1,0:T(8,128)(2,1)S(1)}, f32[4,144,128]{2,1,0:T(8,128)S(1)}) custom-call(bf16[128,4096]{1,0:T(8,128)(2,1)S(1)} %get-tuple-element.10.lhs, bf16[12,4096,128]{2,1,0:T(8,128)(2,1)S(1)} %bitcast.17, s32[64]{0:T(128)} %lens_hbm.1, bf16[64,512,128]{2,1,0:T(8,128)(2,1)} %bitcast.20, ...), custom_call_target="tpu_custom_call" | custom-call | tf_op jit(solution)/shard_map/attend/pallas_call | solution.py:291
  12.8 2.8 %collective-permute-start.2 = (f32[144,128]{1,0:T(8,128)S(1)}, f32[144,128]{1,0:T(8,128)S(1)}, u32[]{:S(2)}, u32[]{:S(2)}) collective-permute-start(f32[144,128]{1,0:T(8,128)S(1)} %get-tuple-element.17), channel_id=1, source_target_pairs={{0,3},{1,0},{2,1},{3,2},{4,7},{5,4},{6,5},{7,6}} | collective-permute-start | bytes 221192 | tf_op jit(solution)/shard_map/ppermute | solution.py:306
  15.6 0.6 %collective-permute-start.1 = (f32[144,128]{1,0:T(8,128)S(1)}, f32[144,128]{1,0:T(8,128)S(1)}, u32[]{:S(2)}, u32[]{:S(2)}) collective-permute-start(f32[144,128]{1,0:T(8,128)S(1)} %get-tuple-element.18), channel_id=1, source_target_pairs={{0,2},{1,3},{2,0},{3,1},{4,6},{5,7},{6,4},{7,5}} | collective-permute-start | bytes 221192 | tf_op jit(solution)/shard_map/ppermute | solution.py:306
  16.2 0.2 collective-permute-start
  16.4 0.0 copy-start
  16.4 6.8 %write.1 = (bf16[64,512,128]{2,1,0:T(8,128)(2,1)}, bf16[64,512,128]{2,1,0:T(8,128)(2,1)}) custom-call(bf16[64,512,128]{2,1,0:T(8,128)(2,1)S(1)} %get-tuple-element.13.k_buf, bf16[64,512,128]{2,1,0:T(8,128)(2,1)S(1)} %get-tuple-element.14.v_buf), custom_call_target="tpu_custom_call" | custom-call | flops 6000000000 | bytes 16777216 | tf_op jit(solution)/shard_map/write/pallas_call | solution.py:307
  23.1 0.0 collective-permute-done.2.o3
  23.1 0.0 collective-permute-done.1.o2
  23.2 0.0 collective-permute-done.o1
  23.2 0.0 copy-done
  23.2 19.1 %rest.1 = bf16[64,2048]{1,0:T(8,128)(2,1)S(1)} custom-call(f32[144,128]{1,0:T(8,128)S(1)} %get-tuple-element.20.o0, f32[144,128]{1,0:T(8,128)S(1)} %collective-permute-done.o1, f32[144,128]{1,0:T(8,128)S(1)} %collective-permute-done.1.o2, f32[144,128]{1,0:T(8,128)S(1)} %collective-permute-done.2.o3, bf16[1024,2048]{1,0:T(8,128)(2,1)S(1)} %bitcast.18, ...), custom_call_target="tpu_custom_call" | custom-call | flops 10000000000 | bytes 20971520 | tf_op jit(solution)/shard_map/rest/pallas_call | solution.py:317
  42.2 0.7 %copy.14 = bf16[64,2048]{1,0:T(8,128)(2,1)} copy(bf16[64,2048]{1,0:T(8,128)(2,1)S(1)} %rest.1) | data formatting | bytes 524288
  (1 shorter events, 0.0 us)
Async XLA Ops:
  12.8 10.4 %collective-permute-start.2 = (f32[144,128]{1,0:T(8,128)S(1)}, f32[144,128]{1,0:T(8,128)S(1)}, u32[]{:S(2)}, u32[]{:S(2)}) collective-permute-start(f32[144,128]{1,0:T(8,128)S(1)} %get-tuple-element.17), channel_id=1, source_target_pairs={{0,3},{1,0},{2,1},{3,2},{4,7},{5,4},{6,5},{7,6}} | collective-permute-start | bytes 221192 | tf_op jit(solution)/shard_map/ppermute | solution.py:306
  15.6 7.6 %collective-permute-start.1 = (f32[144,128]{1,0:T(8,128)S(1)}, f32[144,128]{1,0:T(8,128)S(1)}, u32[]{:S(2)}, u32[]{:S(2)}) collective-permute-start(f32[144,128]{1,0:T(8,128)S(1)} %get-tuple-element.18), channel_id=1, source_target_pairs={{0,2},{1,3},{2,0},{3,1},{4,6},{5,7},{6,4},{7,5}} | collective-permute-start | bytes 221192 | tf_op jit(solution)/shard_map/ppermute | solution.py:306
  16.2 7.0 %collective-permute-start = (f32[144,128]{1,0:T(8,128)S(1)}, f32[144,128]{1,0:T(8,128)S(1)}, u32[]{:S(2)}, u32[]{:S(2)}) collective-permute-start(f32[144,128]{1,0:T(8,128)S(1)} %get-tuple-element.19), channel_id=1, source_target_pairs={{0,1},{1,2},{2,3},{3,0},{4,5},{5,6},{6,7},{7,4}} | collective-permute-start | bytes 221192 | tf_op jit(solution)/shard_map/ppermute | solution.py:306
  16.4 6.8 %copy-start = (bf16[8,128,2048]{2,1,0:T(8,128)(2,1)S(1)}, bf16[8,128,2048]{2,1,0:T(8,128)(2,1)}, u32[]{:S(2)}) copy-start(bf16[8,128,2048]{2,1,0:T(8,128)(2,1)} %param.16) | copy-start | bytes 12582916
